TPU v7x, 256 devices: a whole 4x4x8 slice. The times are simulated.
256 devices in a mesh: gx: 4 (over z_lo), gy: 4 (over y), gz: 16 (over x, z_hi, core).
Axes of the slice: x: 4, y: 4, z: 8 (z_hi: 2, z_lo: 4; z = z_hi * 4 + z_lo), core: 2. Of those that a mesh axis runs over, the one named last changes fastest.
Arguments:
- factor_inv: bfloat16 [4, 4096, 16384], P('gx', 'gy', 'gz')
- sep_sizes: int32 [4, 4, 16], P('gx', 'gy', 'gz'), may hold values from 512 to 1024
- coupling: bfloat16 [12, 4096, 16384], P('gx', 'gy', 'gz'), may hold values from -0.109375 to 0.109375
Outputs:
- schur_update: float32 [4, 4096, 16384], P('gx', 'gy', 'gz')
All inputs are finite; a program needn't handle non-finite values.
Results may differ from a plain program's by a relative error of at most 0.0023.
Values may be sent and summed in bfloat16 or wider, within the bound.
No kernel may reach another device: no remote copies, remote signals or barrier semaphores. Data moves between devices by JAX's collectives and lax.ppermute only.
A program may use at most 128 MiB of HBM per device.

v0:
```python
import jax
import jax.numpy as jnp
from jax import lax
from jax.sharding import PartitionSpec as P


def passed_along(block, axis, distance):
    devices = range(lax.axis_size(axis))
    route = [(i - distance, i) for i in devices if i - distance in devices]
    return lax.ppermute(block, axis, route)


def square_of(solved):
    return lax.dot_general(
        solved, solved, (((0,), (0,)), ((), ())), preferred_element_type=jnp.float32
    )


def update_of(factor, couple):
    solved = jnp.dot(factor, couple, preferred_element_type=jnp.float32).astype(jnp.bfloat16)
    return square_of(solved)


def on_device(factor_inv, sep_sizes, coupling):
    width = factor_inv.shape[1]
    inner = jnp.arange(width, dtype=jnp.int32)
    keep = (inner < sep_sizes[0, 0, 0]).astype(jnp.bfloat16)
    masked = factor_inv[0] * keep[:, None] * keep[None, :]
    below_z = passed_along(masked, "gz", 1)
    above_z = passed_along(masked, "gz", -1)
    below_y = passed_along(masked, "gy", 1)
    total = update_of(below_z, coupling[0])
    total = total + update_of(above_z, coupling[1])
    total = total + update_of(below_y, coupling[2])
    return total[None]


def solution(mesh):
    return jax.shard_map(
        on_device,
        mesh=mesh,
        in_specs=(P("gx", "gy", "gz"), P("gx", "gy", "gz"), P("gx", "gy", "gz")),
        out_specs=P("gx", "gy", "gz"),
        check_vma=False,
    )
```

profile of v0, /device:TPU:197, one launch (start us, length us, event | category | flops | bytes accessed | tf_op | source)
XLA Modules:
  0.0 132.7 jit_solution(6516174092609081375)
XLA Ops:
  0.7 1.8 %fusion.6 = bf16[1024,1024]{1,0:T(8,128)(2,1)S(1)} fusion(bf16[1,1024,1024]{2,1,0:T(8,128)(2,1)} %param.3, bf16[1024]{0:T(1024)(128)(2,1)S(1)} %fusion.30), kind=kLoop, calls=%fused_computation.8 | loop fusion | flops 2097152 | bytes 4196352 | tf_op jit(solution)/shard_map/mul | solution.py:28
  2.5 4.5 %collective-permute-start.2 = (bf16[1024,1024]{1,0:T(8,128)(2,1)S(1)}, bf16[1024,1024]{1,0:T(8,128)(2,1)}, u32[]{:S(2)}, u32[]{:S(2)}) collective-permute-start(bf16[1024,1024]{1,0:T(8,128)(2,1)S(1)} %fusion.6), channel_id=1, source_target_pairs={{0,16},{16,32},{32,48},{1,17},{17,33},{33,49},{2,18},{18,34},{34,5... | collective-permute-start | bytes 6291464 | tf_op jit(solution)/shard_map/ppermute | solution.py:10
  7.1 2.9 %collective-permute-start.1 = (bf16[1024,1024]{1,0:T(8,128)(2,1)S(1)}, bf16[1024,1024]{1,0:T(8,128)(2,1)}, u32[]{:S(2)}, u32[]{:S(2)}) collective-permute-start(bf16[1024,1024]{1,0:T(8,128)(2,1)S(1)} %fusion.6), channel_id=1, source_target_pairs={{1,0},{2,1},{3,2},{4,3},{5,4},{6,5},{7,6},{8,7},{9,8},{10,9},{11,1... | collective-permute-start | bytes 6291464 | tf_op jit(solution)/shard_map/ppermute | solution.py:10
  9.9 7.5 %collective-permute-start = (bf16[1024,1024]{1,0:T(8,128)(2,1)S(1)}, bf16[1024,1024]{1,0:T(8,128)(2,1)}, u32[]{:S(2)}, u32[]{:S(2)}) collective-permute-start(bf16[1024,1024]{1,0:T(8,128)(2,1)S(1)} %fusion.6), channel_id=1, source_target_pairs={{0,1},{1,2},{2,3},{3,4},{4,5},{5,6},{6,7},{7,8},{8,9},{9,10},{10,1... | collective-permute-start | bytes 6291464 | tf_op jit(solution)/shard_map/ppermute | solution.py:10
  17.4 32.6 %collective-permute-done.2 = bf16[1024,1024]{1,0:T(8,128)(2,1)} collective-permute-done((bf16[1024,1024]{1,0:T(8,128)(2,1)S(1)}, bf16[1024,1024]{1,0:T(8,128)(2,1)}, u32[]{:S(2)}, u32[]{:S(2)}) %collective-permute-start.2) | collective-permute-done | bytes 2097184 | tf_op jit(solution)/shard_map/ppermute | solution.py:10
  50.0 12.2 %fusion.7 = f32[1024,1024]{1,0:T(8,128)} fusion(bf16[1024,1024]{1,0:T(8,128)(2,1)} %collective-permute-done.2, bf16[3,1024,1024]{2,1,0:T(8,128)(2,1)} %param.5), kind=kOutput, calls=%fused_computation.9 | convolution fusion | flops 4296015872 | bytes 8388608 | tf_op jit(solution)/shard_map/dot_general | solution.py:14
  62.2 43.5 %collective-permute-done.1 = bf16[1024,1024]{1,0:T(8,128)(2,1)} collective-permute-done((bf16[1024,1024]{1,0:T(8,128)(2,1)S(1)}, bf16[1024,1024]{1,0:T(8,128)(2,1)}, u32[]{:S(2)}, u32[]{:S(2)}) %collective-permute-start.1) | collective-permute-done | bytes 2097184 | tf_op jit(solution)/shard_map/ppermute | solution.py:10
  105.7 12.2 %fusion.10 = f32[1024,1024]{1,0:T(8,128)} fusion(bf16[1024,1024]{1,0:T(8,128)(2,1)} %collective-permute-done.1, bf16[3,1024,1024]{2,1,0:T(8,128)(2,1)} %param.5), kind=kOutput, calls=%fused_computation.12 | convolution fusion | flops 4296015872 | bytes 8388608 | tf_op jit(solution)/shard_map/dot_general | solution.py:14
  117.9 0.0 collective-permute-done
  117.9 14.8 %add_bitcast_fusion = f32[1,1024,1024]{2,1,0:T(8,128)} fusion(f32[1024,1024]{1,0:T(8,128)} %fusion.7, f32[1024,1024]{1,0:T(8,128)} %fusion.10, bf16[1024,1024]{1,0:T(8,128)(2,1)} %collective-permute-done, bf16[3,1024,1024]{2,1,0:T(8,128)(2,1)} %param.5), kind=kOutput, calls=%fused_computation | convolution fusion | flops 4298113024 | bytes 16777216 | tf_op jit(solution)/shard_map/dot_general | solution.py:14
  (1 shorter events, 0.0 us)
Async XLA Ops:
  2.5 47.5 %collective-permute-start.2 = (bf16[1024,1024]{1,0:T(8,128)(2,1)S(1)}, bf16[1024,1024]{1,0:T(8,128)(2,1)}, u32[]{:S(2)}, u32[]{:S(2)}) collective-permute-start(bf16[1024,1024]{1,0:T(8,128)(2,1)S(1)} %fusion.6), channel_id=1, source_target_pairs={{0,16},{16,32},{32,48},{1,17},{17,33},{33,49},{2,18},{18,34},{34,5... | collective-permute-start | bytes 6291464 | tf_op jit(solution)/shard_map/ppermute | solution.py:10
  7.1 98.7 %collective-permute-start.1 = (bf16[1024,1024]{1,0:T(8,128)(2,1)S(1)}, bf16[1024,1024]{1,0:T(8,128)(2,1)}, u32[]{:S(2)}, u32[]{:S(2)}) collective-permute-start(bf16[1024,1024]{1,0:T(8,128)(2,1)S(1)} %fusion.6), channel_id=1, source_target_pairs={{1,0},{2,1},{3,2},{4,3},{5,4},{6,5},{7,6},{8,7},{9,8},{10,9},{11,1... | collective-permute-start | bytes 6291464 | tf_op jit(solution)/shard_map/ppermute | solution.py:10
  9.9 108.0 %collective-permute-start = (bf16[1024,1024]{1,0:T(8,128)(2,1)S(1)}, bf16[1024,1024]{1,0:T(8,128)(2,1)}, u32[]{:S(2)}, u32[]{:S(2)}) collective-permute-start(bf16[1024,1024]{1,0:T(8,128)(2,1)S(1)} %fusion.6), channel_id=1, source_target_pairs={{0,1},{1,2},{2,3},{3,4},{4,5},{5,6},{6,7},{7,8},{8,9},{9,10},{10,1... | collective-permute-start | bytes 6291464 | tf_op jit(solution)/shard_map/ppermute | solution.py:10
where the time goes:
time: 133 us
  waiting for transfers between devices  76.1 us (57%)
  matrix products  39.1 us (29%)
  starting transfers between devices  14.9 us (11%)
  other arithmetic  1.85 us (1%)
    ppermute x3, waiting for transfers between devices, passed_along(): return lax.ppermute(block, axis, route)  76.1 us
    dot_general x3, matrix products, square_of(): lax.dot_general(solved, solved, (((0,), (0,)), ((), ())), preferred_eleme...  39.1 us
    ppermute x3, starting transfers between devices, passed_along(): return lax.ppermute(block, axis, route)  14.9 us
  transfers between devices with their start and end apart: 3, of which 2 were waited for; matrix products, arithmetic and copies ran while one was open for 18% of the time, Pallas kernels for 0%

commit v1 on v0

v1 whole, which is shorter than its diff:
```python
import functools

import jax
import jax.numpy as jnp
from jax import lax
from jax.experimental import pallas as pl
from jax.experimental.pallas import tpu as pltpu
from jax.sharding import PartitionSpec as P


B = 128
EXTRA = 8
UNITS_FIRST = (0, 1, 2)
UNITS_LAST = (3,)


def pack_kernel(size_ref, f_ref, first_ref, last_ref, full_ref):
    count = size_ref[0, 0, 0]
    n = f_ref.shape[1] // B
    width = n * B
    i = lax.broadcasted_iota(jnp.int32, (B, B), 0)
    j = lax.broadcasted_iota(jnp.int32, (B, B), 1)
    row = lax.broadcasted_iota(jnp.int32, (B, 1), 0)
    diags = []
    for u in range(n // 2):
        big = n - 1 - u
        out, at = (first_ref, EXTRA + B * UNITS_FIRST.index(u)) if u in UNITS_FIRST else (last_ref, B * UNITS_LAST.index(u))
        keep_big = (row + big * B) < count
        keep_small = (row + u * B) < count
        rows_big = f_ref[0, big * B:(big + 1) * B, :]
        rows_big = jnp.where(keep_big, rows_big, jnp.zeros_like(rows_big))
        rows_small = f_ref[0, u * B:(u + 1) * B, :]
        rows_small = jnp.where(keep_small, rows_small, jnp.zeros_like(rows_small))
        d_big = rows_big[:, big * B:(big + 1) * B].astype(jnp.float32)
        d_small = rows_small[:, u * B:(u + 1) * B].astype(jnp.float32)
        square = jnp.where(i >= j, d_small, d_big.T).astype(jnp.bfloat16)
        diags.append(jnp.sum(jnp.where(i == j, d_big, 0.0), axis=0, keepdims=True))
        for ref, to in ((out, at), (full_ref, EXTRA + B * u)):
            ref[to:to + B, 0:big * B] = rows_big[:, 0:big * B]
            ref[to:to + B, big * B:(big + 1) * B] = square
            if u:
                ref[to:to + B, (big + 1) * B:width] = rows_small[:, 0:u * B]
    line = jnp.concatenate(diags + [jnp.zeros((1, width - B * len(diags)), jnp.float32)], axis=1)
    line = jnp.broadcast_to(line, (EXTRA, width)).astype(jnp.bfloat16)
    first_ref[0:EXTRA, :] = line
    full_ref[0:EXTRA, :] = line


def packed(factor_inv, sep_sizes):
    width = factor_inv.shape[1]
    first = EXTRA + B * len(UNITS_FIRST)
    last = B * len(UNITS_LAST)
    return pl.pallas_call(
        pack_kernel,
        out_shape=(
            jax.ShapeDtypeStruct((first, width), jnp.bfloat16),
            jax.ShapeDtypeStruct((last, width), jnp.bfloat16),
            jax.ShapeDtypeStruct((first + last, width), jnp.bfloat16),
        ),
        in_specs=[
            pl.BlockSpec(memory_space=pltpu.SMEM),
            pl.BlockSpec(memory_space=pltpu.VMEM),
        ],
        out_specs=(pl.BlockSpec(memory_space=pltpu.VMEM),) * 3,
        compiler_params=pltpu.CompilerParams(vmem_limit_bytes=12 << 20),
        cost_estimate=pl.CostEstimate(flops=4 * width * width, bytes_accessed=3 * width * width, transcendentals=0),
        name="pack",
    )(sep_sizes, factor_inv)


def place(g, at, unit, u, diag, n):
    i = lax.broadcasted_iota(jnp.int32, (B, B), 0)
    j = lax.broadcasted_iota(jnp.int32, (B, B), 1)
    big = n - 1 - u
    square = unit[:, big * B:(big + 1) * B].astype(jnp.float32)
    lower = jnp.where(i >= j, square, 0.0).astype(jnp.bfloat16)
    line = diag[:, u * B:(u + 1) * B].astype(jnp.float32)
    other = jnp.where(i > j, square.T, jnp.where(i == j, line, 0.0)).astype(jnp.bfloat16)
    lo, hi = at
    if u:
        g[lo:lo + B, 0:u * B] = unit[:, (big + 1) * B:n * B]
    g[lo:lo + B, u * B:(u + 1) * B] = lower
    g[hi:hi + B, 0:big * B] = unit[:, 0:big * B]
    g[hi:hi + B, big * B:(big + 1) * B] = other


def slot_kernel(units, has_acc, which_ref, *refs):
    which = which_ref[0]
    if has_acc:
        acc_ref, *refs = refs
    c_ref, *parts, out_ref, g, x = refs
    first_ref = parts[0]
    n = c_ref.shape[1] // B
    panels = sorted([u for u in units] + [n - 1 - u for u in units])
    where = {p: k * B for k, p in enumerate(panels)}

    @pl.when(pl.program_id(0) == 0)
    def _():
        diag = first_ref[0:1, :]
        g[...] = jnp.zeros_like(g)
        for u in units:
            if len(parts) == 1:
                at = EXTRA + B * u
                unit = first_ref[at:at + B, :]
            else:
                at = B * UNITS_LAST.index(u)
                unit = parts[1][at:at + B, :]
            place(g, (where[u], where[n - 1 - u]), unit, u, diag, n)
        for k in range(0, len(panels), 2):
            depth = (panels[k + 1] + 1) * B
            x[k * B:(k + 2) * B, :] = jnp.dot(
                g[k * B:(k + 2) * B, 0:depth], c_ref[which, 0:depth, :], preferred_element_type=jnp.float32
            ).astype(jnp.bfloat16)

    wide = out_ref.shape[-1]
    cols = pl.ds(pl.multiple_of(pl.program_id(0) * wide, wide), wide)
    part = lax.dot_general(
        x[...], x[:, cols], (((0,), (0,)), ((), ())), preferred_element_type=jnp.float32
    )
    if has_acc:
        part = part + acc_ref[0, :, cols]
    out_ref[0] = part


def update(which, coupling, parts, units, acc):
    width = coupling.shape[1]
    rows = 2 * B * len(units)
    steps = 4
    wide = width // steps
    block = pl.BlockSpec((1, width, wide), lambda s, w: (0, 0, s))
    held = pl.BlockSpec(memory_space=pltpu.VMEM)
    ins = ([acc] if acc is not None else []) + [coupling, *parts]
    specs = [held] * len(ins)
    return pl.pallas_call(
        functools.partial(slot_kernel, units, acc is not None),
        out_shape=jax.ShapeDtypeStruct((1, width, width), jnp.float32),
        grid_spec=pltpu.PrefetchScalarGridSpec(
            num_scalar_prefetch=1,
            grid=(steps,),
            in_specs=specs,
            out_specs=block,
            scratch_shapes=[
                pltpu.VMEM((rows, width), jnp.bfloat16),
                pltpu.VMEM((rows, width), jnp.bfloat16),
            ],
        ),
        cost_estimate=pl.CostEstimate(
            flops=4 * rows * width * width, bytes_accessed=10 * width * width, transcendentals=0
        ),
        compiler_params=pltpu.CompilerParams(vmem_limit_bytes=24 << 20),
    )(which, *ins)


def on_device(factor_inv, sep_sizes, coupling):
    first, last, full = packed(factor_inv, sep_sizes)
    n_z = lax.axis_size("gz")
    n_y = lax.axis_size("gy")
    far_pairs = [p for k in range(1, n_z - 1, 2) for p in ((k, k + 1), (k + 1, k))]
    near_pairs = [p for k in range(0, n_z, 2) for p in ((k, k + 1), (k + 1, k))]
    up = [(k, k + 1) for k in range(n_y - 1)]
    far_first = lax.ppermute(first, "gz", far_pairs)
    far_last = lax.ppermute(last, "gz", far_pairs)
    near = lax.ppermute(full, "gz", near_pairs)
    below_y = lax.ppermute(full, "gy", up)

    odd = lax.axis_index("gz") % 2
    far_slot = jnp.reshape(odd, (1,)).astype(jnp.int32)
    near_slot = 1 - far_slot
    y_slot = jnp.full((1,), 2, jnp.int32)
    every = UNITS_FIRST + UNITS_LAST
    total = update(near_slot, coupling, (near,), every, None)
    total = update(y_slot, coupling, (below_y,), every, total)
    total = update(far_slot, coupling, (far_first,), UNITS_FIRST, total)
    return update(far_slot, coupling, (far_first, far_last), UNITS_LAST, total)


def solution(mesh):
    return jax.shard_map(
        on_device,
        mesh=mesh,
        in_specs=(P("gx", "gy", "gz"), P("gx", "gy", "gz"), P("gx", "gy", "gz")),
        out_specs=P("gx", "gy", "gz"),
        check_vma=False,
    )
```

time: 133 us -> 73 us (0.55)
  the two profiles are of different devices: /device:TPU:197 before, /device:TPU:6 now
where the time goes in v1:
time: 73 us; the launch traced here: 72.8 us
  waiting for transfers between devices  32.5 us (45%)
  Pallas kernels  20.6 us (28%)
  starting transfers between devices  14.7 us (20%)
  local copies, waits for them, and re-layouts  4.37 us (6%)
  between operations  0.75 us (1%)
    ppermute x1, waiting for transfers between devices, on_device(): far_first = lax.ppermute(first, 'gz', far_pairs)  29.6 us
    pallas_call x4, Pallas kernels, update(): pl.pallas_call(functools.partial(slot_kernel, units, acc is not None), ou...  19.5 us
    ppermute x1, starting transfers between devices, on_device(): far_last = lax.ppermute(last, 'gz', far_pairs)  9.19 us
    unnamed x6, local copies, waits for them, and re-layouts  4.37 us
    ppermute x1, starting transfers between devices, on_device(): below_y = lax.ppermute(full, 'gy', up)  3.54 us
    ppermute x1, waiting for transfers between devices, on_device(): below_y = lax.ppermute(full, 'gy', up)  2.89 us
    ppermute x1, starting transfers between devices, on_device(): far_first = lax.ppermute(first, 'gz', far_pairs)  1.92 us
  transfers between devices with their start and end apart: 4, of which 2 were waited for; matrix products, arithmetic and copies ran while one was open for 0% of the time, Pallas kernels for 22%

profile of v1, /device:TPU:6, one launch (start us, length us, event | category | flops | bytes accessed | tf_op | source)
XLA Modules:
  0.0 72.8 jit_solution(5455102444931473641)
XLA Ops:
  0.7 0.0 copy-start.2
  0.7 1.6 %copy-done.2 = bf16[1,1024,1024]{2,1,0:T(8,128)(2,1)S(1)} copy-done((bf16[1,1024,1024]{2,1,0:T(8,128)(2,1)S(1)}, bf16[1,1024,1024]{2,1,0:T(8,128)(2,1)}, u32[]{:S(2)}) %copy-start.2) | copy-done | bytes 2097176
  2.2 1.1 %pack.1 = (bf16[392,1024]{1,0:T(8,128)(2,1)}, bf16[128,1024]{1,0:T(8,128)(2,1)S(1)}, bf16[520,1024]{1,0:T(8,128)(2,1)S(1)}) custom-call(s32[1,1,1]{2,1,0:T(1,128)S(6)} %copy.4.size_ref, bf16[1,1024,1024]{2,1,0:T(8,128)(2,1)S(1)} %copy-done.2), custom_call_target="tpu_custom_call" | custom-call | flops 4194304 | bytes 3145728 | tf_op jit(solution)/shard_map/pack/pallas_call | solution.py:53
  3.4 0.0 collective-permute-start
  3.4 3.5 %collective-permute-start.1 = (bf16[520,1024]{1,0:T(8,128)(2,1)S(1)}, bf16[520,1024]{1,0:T(8,128)(2,1)S(1)}, u32[]{:S(2)}, u32[]{:S(2)}) collective-permute-start(bf16[520,1024]{1,0:T(8,128)(2,1)S(1)} %get-tuple-element.8), channel_id=1, source_target_pairs={{0,16},{16,32},{32,48},{1,17},{17,33},{33,49},{2,18},{18,34},{34,5... | collective-permute-start | bytes 3194888 | tf_op jit(solution)/shard_map/ppermute | solution.py:164
  6.9 9.2 %collective-permute-start.3 = (bf16[128,1024]{1,0:T(8,128)(2,1)S(1)}, bf16[128,1024]{1,0:T(8,128)(2,1)S(1)}, u32[]{:S(2)}, u32[]{:S(2)}) collective-permute-start(bf16[128,1024]{1,0:T(8,128)(2,1)S(1)} %get-tuple-element.10), channel_id=1, source_target_pairs={{1,2},{2,1},{3,4},{4,3},{5,6},{6,5},{7,8},{8,7},{9,10},{10,9},{11,... | collective-permute-start | bytes 786440 | tf_op jit(solution)/shard_map/ppermute | solution.py:162
  16.1 1.9 %collective-permute-start.2 = (bf16[392,1024]{1,0:T(8,128)(2,1)}, bf16[392,1024]{1,0:T(8,128)(2,1)S(1)}, u32[]{:S(2)}, u32[]{:S(2)}) collective-permute-start(bf16[392,1024]{1,0:T(8,128)(2,1)} %get-tuple-element.9), channel_id=1, source_target_pairs={{1,2},{2,1},{3,4},{4,3},{5,6},{6,5},{7,8},{8,7},{9,10},{10,9},{11,... | collective-permute-start | bytes 2408456 | tf_op jit(solution)/shard_map/ppermute | solution.py:161
  18.1 0.0 collective-permute-done.refs_1_
  18.1 0.0 copy-start
  18.1 2.8 %copy-done = bf16[3,1024,1024]{2,1,0:T(8,128)(2,1)S(1)} copy-done((bf16[3,1024,1024]{2,1,0:T(8,128)(2,1)S(1)}, bf16[3,1024,1024]{2,1,0:T(8,128)(2,1)}, u32[]{:S(2)}) %copy-start) | copy-done | bytes 6291480
  20.8 0.0 copy-start.1
  20.9 6.5 %shard_map.37.refs_0_ = f32[1,1024,1024]{2,1,0:T(8,128)S(1)} custom-call(s32[1]{0:T(128)S(6)} %sub.3.which_ref, bf16[3,1024,1024]{2,1,0:T(8,128)(2,1)S(1)} %copy-done, bf16[520,1024]{1,0:T(8,128)(2,1)} %collective-permute-done.refs_1_), custom_call_target="tpu_custom_call" | custom-call | flops 4294967296 | bytes 10485760 | tf_op jit(solution)/shard_map/pallas_call | solution.py:134
  27.4 2.9 %collective-permute-done.1.refs_2_ = bf16[520,1024]{1,0:T(8,128)(2,1)S(1)} collective-permute-done((bf16[520,1024]{1,0:T(8,128)(2,1)S(1)}, bf16[520,1024]{1,0:T(8,128)(2,1)S(1)}, u32[]{:S(2)}, u32[]{:S(2)}) %collective-permute-start.1) | collective-permute-done | bytes 1064992 | tf_op jit(solution)/shard_map/ppermute | solution.py:164
  30.3 0.0 copy-done.1
  30.3 5.1 %shard_map.38.refs_0_ = f32[1,1024,1024]{2,1,0:T(8,128)S(1)} custom-call(s32[1]{0:T(128)} %constant.19.clone.1.which_ref, f32[1,1024,1024]{2,1,0:T(8,128)S(1)} %shard_map.37.refs_0_, bf16[3,1024,1024]{2,1,0:T(8,128)(2,1)S(1)} %copy-done.1, bf16[520,1024]{1,0:T(8,128)(2,1)S(1)} %collective-permute-done.1.refs_2_), custom_call_target="tpu_custom_call" | custom-call | flops 4294967296 | bytes 10485760 | tf_op jit(solution)/shard_map/pallas_call | solution.py:134
  35.3 29.6 %collective-permute-done.2.refs_2_ = bf16[392,1024]{1,0:T(8,128)(2,1)S(1)} collective-permute-done((bf16[392,1024]{1,0:T(8,128)(2,1)}, bf16[392,1024]{1,0:T(8,128)(2,1)S(1)}, u32[]{:S(2)}, u32[]{:S(2)}) %collective-permute-start.2) | collective-permute-done | bytes 802848 | tf_op jit(solution)/shard_map/ppermute | solution.py:161
  64.9 4.2 %shard_map.39.refs_0_ = f32[1,1024,1024]{2,1,0:T(8,128)S(1)} custom-call(s32[1]{0:T(128)} %bitcast.which_ref, f32[1,1024,1024]{2,1,0:T(8,128)S(1)} %shard_map.38.refs_0_, bf16[3,1024,1024]{2,1,0:T(8,128)(2,1)S(1)} %copy-done.1, bf16[392,1024]{1,0:T(8,128)(2,1)S(1)} %collective-permute-done.2.refs_2_), custom_call_target="tpu_custom_call" | custom-call | flops 3221225472 | bytes 10485760 | tf_op jit(solution)/shard_map/pallas_call | solution.py:134
  69.2 0.0 collective-permute-done.3.refs_3_
  69.2 3.6 %shard_map.40 = f32[1,1024,1024]{2,1,0:T(8,128)} custom-call(s32[1]{0:T(128)} %bitcast.which_ref, f32[1,1024,1024]{2,1,0:T(8,128)S(1)} %shard_map.39.refs_0_, bf16[3,1024,1024]{2,1,0:T(8,128)(2,1)S(1)} %copy-done.1, bf16[392,1024]{1,0:T(8,128)(2,1)S(1)} %collective-permute-done.2.refs_2_, bf16[128,1024]{1,0:T(8,128)(2,1)S(1)} %collective-permute-done.3.refs_3_), custom_call_target="tpu_custom_call" | custom-call | flops 1073741824 | bytes 10485760 | tf_op jit(solution)/shard_map/pallas_call | solution.py:134
Async XLA Ops:
  0.7 1.6 %copy-start.2 = (bf16[1,1024,1024]{2,1,0:T(8,128)(2,1)S(1)}, bf16[1,1024,1024]{2,1,0:T(8,128)(2,1)}, u32[]{:S(2)}) copy-start(bf16[1,1024,1024]{2,1,0:T(8,128)(2,1)} %f_ref.1) | copy-start | bytes 6291460
  3.4 14.7 %collective-permute-start = (bf16[520,1024]{1,0:T(8,128)(2,1)S(1)}, bf16[520,1024]{1,0:T(8,128)(2,1)}, u32[]{:S(2)}, u32[]{:S(2)}) collective-permute-start(bf16[520,1024]{1,0:T(8,128)(2,1)S(1)} %get-tuple-element.8), channel_id=1, source_target_pairs={{0,1},{1,0},{2,3},{3,2},{4,5},{5,4},{6,7},{7,6},{8,9},{9,8},{10,11... | collective-permute-start | bytes 3194888 | tf_op jit(solution)/shard_map/ppermute | solution.py:163
  3.4 26.9 %collective-permute-start.1 = (bf16[520,1024]{1,0:T(8,128)(2,1)S(1)}, bf16[520,1024]{1,0:T(8,128)(2,1)S(1)}, u32[]{:S(2)}, u32[]{:S(2)}) collective-permute-start(bf16[520,1024]{1,0:T(8,128)(2,1)S(1)} %get-tuple-element.8), channel_id=1, source_target_pairs={{0,16},{16,32},{32,48},{1,17},{17,33},{33,49},{2,18},{18,34},{34,5... | collective-permute-start | bytes 3194888 | tf_op jit(solution)/shard_map/ppermute | solution.py:164
  6.9 62.3 %collective-permute-start.3 = (bf16[128,1024]{1,0:T(8,128)(2,1)S(1)}, bf16[128,1024]{1,0:T(8,128)(2,1)S(1)}, u32[]{:S(2)}, u32[]{:S(2)}) collective-permute-start(bf16[128,1024]{1,0:T(8,128)(2,1)S(1)} %get-tuple-element.10), channel_id=1, source_target_pairs={{1,2},{2,1},{3,4},{4,3},{5,6},{6,5},{7,8},{8,7},{9,10},{10,9},{11,... | collective-permute-start | bytes 786440 | tf_op jit(solution)/shard_map/ppermute | solution.py:162
  16.1 48.8 %collective-permute-start.2 = (bf16[392,1024]{1,0:T(8,128)(2,1)}, bf16[392,1024]{1,0:T(8,128)(2,1)S(1)}, u32[]{:S(2)}, u32[]{:S(2)}) collective-permute-start(bf16[392,1024]{1,0:T(8,128)(2,1)} %get-tuple-element.9), channel_id=1, source_target_pairs={{1,2},{2,1},{3,4},{4,3},{5,6},{6,5},{7,8},{8,7},{9,10},{10,9},{11,... | collective-permute-start | bytes 2408456 | tf_op jit(solution)/shard_map/ppermute | solution.py:161
  18.1 2.8 %copy-start = (bf16[3,1024,1024]{2,1,0:T(8,128)(2,1)S(1)}, bf16[3,1024,1024]{2,1,0:T(8,128)(2,1)}, u32[]{:S(2)}) copy-start(bf16[3,1024,1024]{2,1,0:T(8,128)(2,1)} %refs_1_.5) | copy-start | bytes 18874372
  20.8 9.4 %copy-start.1 = (bf16[3,1024,1024]{2,1,0:T(8,128)(2,1)S(1)}, bf16[3,1024,1024]{2,1,0:T(8,128)(2,1)}, u32[]{:S(2)}) copy-start(bf16[3,1024,1024]{2,1,0:T(8,128)(2,1)} %refs_1_.5) | copy-start | bytes 18874372

commit v2 on v1

v2 whole, which is shorter than its diff:
```python
import functools

import jax
import jax.numpy as jnp
from jax import lax
from jax.experimental import pallas as pl
from jax.experimental.pallas import tpu as pltpu
from jax.sharding import PartitionSpec as P


B = 128
EXTRA = 8
UNITS_FIRST = (0, 1, 2)
UNITS_LAST = (3,)


def pack_kernel(size_ref, f_ref, first_ref, last_ref, full_ref, held, sems):
    count = size_ref[0, 0, 0]
    n = f_ref.shape[1] // B
    width = n * B
    i = lax.broadcasted_iota(jnp.int32, (B, B), 0)
    j = lax.broadcasted_iota(jnp.int32, (B, B), 1)
    row = lax.broadcasted_iota(jnp.int32, (B, 1), 0)

    def copy(p):
        spot = (pl.ds(p * B, B), pl.ds(0, (p + 1) * B))
        return pltpu.make_async_copy(f_ref.at[(0, *spot)], held.at[spot], sems.at[p])

    order = [p for u in range(n // 2) for p in (n - 1 - u, u)]
    for p in order:
        copy(p).start()
    diags = []
    for u in range(n // 2):
        big = n - 1 - u
        out, at = (first_ref, EXTRA + B * UNITS_FIRST.index(u)) if u in UNITS_FIRST else (last_ref, B * UNITS_LAST.index(u))
        copy(big).wait()
        copy(u).wait()
        keep_big = (row + big * B) < count
        keep_small = (row + u * B) < count
        rows_big = held[big * B:(big + 1) * B, 0:(big + 1) * B]
        rows_big = jnp.where(keep_big, rows_big, jnp.zeros_like(rows_big))
        rows_small = held[u * B:(u + 1) * B, 0:(u + 1) * B]
        rows_small = jnp.where(keep_small, rows_small, jnp.zeros_like(rows_small))
        d_big = rows_big[:, big * B:(big + 1) * B].astype(jnp.float32)
        d_small = rows_small[:, u * B:(u + 1) * B].astype(jnp.float32)
        square = jnp.where(i >= j, d_small, d_big.T).astype(jnp.bfloat16)
        diags.append(jnp.sum(jnp.where(i == j, d_big, 0.0), axis=0, keepdims=True))
        for ref, to in ((out, at), (full_ref, EXTRA + B * u)):
            ref[to:to + B, 0:big * B] = rows_big[:, 0:big * B]
            ref[to:to + B, big * B:(big + 1) * B] = square
            if u:
                ref[to:to + B, (big + 1) * B:width] = rows_small[:, 0:u * B]
    line = jnp.concatenate(diags + [jnp.zeros((1, width - B * len(diags)), jnp.float32)], axis=1)
    line = jnp.broadcast_to(line, (EXTRA, width)).astype(jnp.bfloat16)
    first_ref[0:EXTRA, :] = line
    full_ref[0:EXTRA, :] = line


def packed(factor_inv, sep_sizes):
    width = factor_inv.shape[1]
    first = EXTRA + B * len(UNITS_FIRST)
    last = B * len(UNITS_LAST)
    return pl.pallas_call(
        pack_kernel,
        out_shape=tuple(pltpu.VMEM((rows, width), jnp.bfloat16) for rows in (first, last, first + last)),
        in_specs=[
            pl.BlockSpec(memory_space=pltpu.SMEM),
            pl.BlockSpec(memory_space=pltpu.HBM),
        ],
        out_specs=(pl.BlockSpec(memory_space=pltpu.VMEM),) * 3,
        scratch_shapes=[pltpu.VMEM((width, width), jnp.bfloat16), pltpu.SemaphoreType.DMA((width // B,))],
        compiler_params=pltpu.CompilerParams(vmem_limit_bytes=60 << 20),
        cost_estimate=pl.CostEstimate(flops=4 * width * width, bytes_accessed=3 * width * width, transcendentals=0),
        name="pack",
    )(sep_sizes, factor_inv)


def place(g, at, unit, u, diag, n):
    i = lax.broadcasted_iota(jnp.int32, (B, B), 0)
    j = lax.broadcasted_iota(jnp.int32, (B, B), 1)
    big = n - 1 - u
    square = unit[:, big * B:(big + 1) * B].astype(jnp.float32)
    lower = jnp.where(i >= j, square, 0.0).astype(jnp.bfloat16)
    line = diag[:, u * B:(u + 1) * B].astype(jnp.float32)
    other = jnp.where(i > j, square.T, jnp.where(i == j, line, 0.0)).astype(jnp.bfloat16)
    lo, hi = at
    if u:
        g[lo:lo + B, 0:u * B] = unit[:, (big + 1) * B:n * B]
    g[lo:lo + B, u * B:(u + 1) * B] = lower
    g[hi:hi + B, 0:big * B] = unit[:, 0:big * B]
    g[hi:hi + B, big * B:(big + 1) * B] = other


def product(x, depth):
    blocks = x.shape[1] // depth
    for b in range(blocks):
        cols = slice(b * depth, (b + 1) * depth)
        low = slice(b * depth, x.shape[1])
        yield b, cols, low, lax.dot_general(
            x[:, low], x[:, cols], (((0,), (0,)), ((), ())), preferred_element_type=jnp.float32
        )


def slot_kernel(units, has_acc, whole, which_ref, *refs):
    if has_acc:
        acc_ref, *refs = refs
    c_ref, part_ref, out_ref, g, x = refs
    which = which_ref[0]
    n = c_ref.shape[1] // B
    panels = sorted([u for u in units] + [n - 1 - u for u in units])
    where = {p: k * B for k, p in enumerate(panels)}
    for k in range(0, len(panels), 2):
        lo, hi = panels[k], panels[k + 1]
        g[k * B:(k + 1) * B, (lo + 1) * B:(hi + 1) * B] = jnp.zeros((B, (hi - lo) * B), jnp.bfloat16)
    diag = part_ref[0:1, :]
    for u in units:
        at = EXTRA + B * u
        place(g, (where[u], where[n - 1 - u]), part_ref[at:at + B, :], u, diag, n)
    wide = 2 * B
    depths = [(panels[k + 1] + 1) * B for k in range(0, len(panels), 2)]
    for b in range(n // 2):
        cols = slice(b * wide, (b + 1) * wide)
        solved, done, start = None, [], 0
        for k, depth in enumerate(depths):
            part = jnp.dot(
                g[k * wide:, start:depth], c_ref[which, start:depth, cols], preferred_element_type=jnp.float32
            )
            solved = part if solved is None else solved[wide:] + part
            done.append(solved[:wide])
            start = depth
        x[:, cols] = jnp.concatenate(done, axis=0).astype(jnp.bfloat16)
    for b, cols, low, part in product(x, wide):
        if has_acc:
            part = part + acc_ref[0, low, cols]
        out_ref[0, low, cols] = part
        if whole:
            for k in range(b + 1, n // 2):
                out_ref[0, cols, k * wide:(k + 1) * wide] = part[(k - b) * wide:(k - b + 1) * wide].T


def update(which, coupling, part, units, acc, whole=False):
    width = coupling.shape[1]
    rows = 2 * B * len(units)
    ins = ([acc] if acc is not None else []) + [coupling, part]
    return pl.pallas_call(
        functools.partial(slot_kernel, units, acc is not None, whole),
        out_shape=jax.ShapeDtypeStruct((1, width, width), jnp.float32),
        in_specs=[pl.BlockSpec(memory_space=pltpu.SMEM)] + [pl.BlockSpec(memory_space=pltpu.VMEM)] * len(ins),
        out_specs=pl.BlockSpec(memory_space=pltpu.VMEM),
        scratch_shapes=[
            pltpu.VMEM((rows, width), jnp.bfloat16),
            pltpu.VMEM((rows, width), jnp.bfloat16),
        ],
        compiler_params=pltpu.CompilerParams(vmem_limit_bytes=24 << 20),
        cost_estimate=pl.CostEstimate(
            flops=4 * rows * width * width, bytes_accessed=10 * width * width, transcendentals=0
        ),
    )(which, *ins)


def last_kernel(which_ref, acc_ref, c_ref, first_ref, *refs):
    last_refs, (out_ref, g, x, sums, sems) = refs[:-5], refs[-5:]
    which = which_ref[0]
    n = c_ref.shape[1] // B
    panels = sorted([u for u in UNITS_LAST] + [n - 1 - u for u in UNITS_LAST])
    where = {p: k * B for k, p in enumerate(panels)}
    for k in range(0, len(panels), 2):
        lo, hi = panels[k], panels[k + 1]
        g[k * B:(k + 1) * B, (lo + 1) * B:(hi + 1) * B] = jnp.zeros((B, (hi - lo) * B), jnp.bfloat16)
    for u in UNITS_LAST:
        at = B * UNITS_LAST.index(u)
        unit = sum((ref[at:at + B, :] for ref in last_refs[1:]), last_refs[0][at:at + B, :])
        place(g, (where[u], where[n - 1 - u]), unit, u, first_ref[0:1, :], n)
    blocks = 4
    wide = n * B // blocks
    cut = [slice(b * wide, (b + 1) * wide) for b in range(blocks)]
    for cols in cut:
        for k in range(0, len(panels), 2):
            depth = (panels[k + 1] + 1) * B
            x[k * B:(k + 2) * B, cols] = jnp.dot(
                g[k * B:(k + 2) * B, 0:depth], c_ref[which, 0:depth, cols], preferred_element_type=jnp.float32
            ).astype(jnp.bfloat16)

    def copy(b):
        cols = pl.ds(b * wide, wide)
        return pltpu.make_async_copy(sums.at[:, cols], out_ref.at[0, :, cols], sems.at[b])

    for b, cols in enumerate(cut):
        part = lax.dot_general(x[...], x[:, cols], (((0,), (0,)), ((), ())), preferred_element_type=jnp.float32)
        sums[:, cols] = acc_ref[0, :, cols] + part
        copy(b).start()
    for b in range(blocks):
        copy(b).wait()


def last_update(which, coupling, parts, acc):
    width = coupling.shape[1]
    rows = 2 * B * len(UNITS_LAST)
    return pl.pallas_call(
        last_kernel,
        out_shape=jax.ShapeDtypeStruct((1, width, width), jnp.float32),
        in_specs=[pl.BlockSpec(memory_space=pltpu.SMEM)] + [pl.BlockSpec(memory_space=pltpu.VMEM)] * (2 + len(parts)),
        out_specs=pl.BlockSpec(memory_space=pltpu.HBM),
        scratch_shapes=[
            pltpu.VMEM((rows, width), jnp.bfloat16),
            pltpu.VMEM((rows, width), jnp.bfloat16),
            pltpu.VMEM((width, width), jnp.float32),
            pltpu.SemaphoreType.DMA((4,)),
        ],
        compiler_params=pltpu.CompilerParams(vmem_limit_bytes=16 << 20),
        cost_estimate=pl.CostEstimate(
            flops=4 * rows * width * width, bytes_accessed=10 * width * width, transcendentals=0
        ),
        name="last",
    )(which, acc, coupling, *parts)


def moved(block, pairs):
    return lax.ppermute(block, ("gx", "gy", "gz"), pairs)


def routes(n_lo, n_y, n_z):
    big, small, near, up = [], [], [], []
    aside, beside, rising, falling = (([], []) for _ in range(4))
    columns = n_z // 4
    for lo in range(n_lo):
        for y in range(n_y):
            at = lambda k: (lo * n_y + y) * n_z + k
            for k in range(0, n_z, 2):
                near += [(at(k), at(k + 1)), (at(k + 1), at(k))]
            if y + 1 < n_y:
                up += [(at(k), at(k) + n_z) for k in range(n_z)]
            for x in range(columns):
                for pair in ((4 * x + 1, 4 * x + 2), (4 * x + 2, 4 * x + 1)):
                    big.append(tuple(map(at, pair)))
                    small.append(tuple(map(at, pair)))
            end = 4 * (columns - 1)
            for x in range(columns - 1):
                right, left = 4 * x + 3, 4 * x + 4
                turn, side = divmod(columns - 2 - x, 2)
                back, other = divmod(x, 2)
                for source, target, relay, first, onward, which in (
                    (right, left, end + 3 - side, aside, rising, turn),
                    (left, right, other, beside, falling, back),
                ):
                    big.append((at(source), at(target)))
                    first[which].append((at(source), at(relay)))
                    onward[which].append((at(relay), at(target)))
    return big, small, aside, rising, beside, falling, near, up


def on_device(factor_inv, sep_sizes, coupling):
    first, last, full = packed(factor_inv, sep_sizes)
    big, small, aside, rising, beside, falling, near_pairs, up = routes(*(lax.axis_size(a) for a in ("gx", "gy", "gz")))
    far_first = moved(first, big)
    side_a = moved(last, aside[0])
    side_b = moved(last, aside[1])
    far_last = moved(last, small)
    rising_a = moved(side_a, rising[0])
    rising_b = moved(side_b, rising[1])
    below_y = moved(full, up)
    side_c = moved(last, beside[0])
    side_d = moved(last, beside[1])
    falling_a = moved(side_c, falling[0])
    falling_b = moved(side_d, falling[1])
    near = moved(full, near_pairs)

    odd = lax.axis_index("gz") % 2
    far_slot = jnp.reshape(odd, (1,)).astype(jnp.int32)
    near_slot = 1 - far_slot
    y_slot = jnp.full((1,), 2, jnp.int32)
    every = UNITS_FIRST + UNITS_LAST
    total = update(near_slot, coupling, near, every, None)
    total = update(y_slot, coupling, below_y, every, total)
    total = update(far_slot, coupling, far_first, UNITS_FIRST, total, whole=True)
    return last_update(far_slot, coupling, (far_first, far_last, rising_a, rising_b, falling_a, falling_b), total)


def solution(mesh):
    return jax.shard_map(
        on_device,
        mesh=mesh,
        in_specs=(P("gx", "gy", "gz"), P("gx", "gy", "gz"), P("gx", "gy", "gz")),
        out_specs=P("gx", "gy", "gz"),
        check_vma=False,
    )
```

time: 73 us -> 82.3 us (1.13)
  the two profiles are of different devices: /device:TPU:6 before, /device:TPU:33 now
where the time goes in v2:
time: 82.3 us; the launch traced here: 82 us
  starting transfers between devices  40.4 us (49%)
  waiting for transfers between devices  23.7 us (29%)
  Pallas kernels  14.2 us (17%)
  local copies, waits for them, and re-layouts  2.78 us (3%)
  between operations  0.83 us (1%)
    ppermute x12, starting transfers between devices, moved(): return lax.ppermute(block, ('gx', 'gy', 'gz'), pairs)  40.4 us
    ppermute x12, waiting for transfers between devices, moved(): return lax.ppermute(block, ('gx', 'gy', 'gz'), pairs)  23.7 us
    pallas_call x3, Pallas kernels, update(): pl.pallas_call(functools.partial(slot_kernel, units, acc is not None, who...  9.65 us
    pallas_call x1, Pallas kernels, last_update(): pl.pallas_call(last_kernel, out_shape=jax.ShapeDtypeStruct((1, width, wid...  3.07 us
    unnamed x4, local copies, waits for them, and re-layouts  2.78 us
  transfers between devices with their start and end apart: 12, of which 3 were waited for; matrix products, arithmetic and copies ran while one was open for 0% of the time, Pallas kernels for 12%

profile of v2, /device:TPU:33, one launch (start us, length us, event | category | flops | bytes accessed | tf_op | source)
XLA Modules:
  0.0 82.0 jit_solution(11819102198196641311)
XLA Ops:
  0.7 1.5 %pack.1 = (bf16[392,1024]{1,0:T(8,128)(2,1)S(1)}, bf16[128,1024]{1,0:T(8,128)(2,1)S(1)}, bf16[520,1024]{1,0:T(8,128)(2,1)S(1)}) custom-call(s32[1,1,1]{2,1,0:T(1,128)S(6)} %copy.4.size_ref, bf16[1,1024,1024]{2,1,0:T(8,128)(2,1)} %f_ref.1), custom_call_target="tpu_custom_call" | custom-call | flops 4194304 | bytes 3145728 | tf_op jit(solution)/shard_map/pack/pallas_call | solution.py:63
  2.2 0.8 collective-permute-start
  2.9 3.3 %collective-permute-start.1 = (bf16[520,1024]{1,0:T(8,128)(2,1)S(1)}, bf16[520,1024]{1,0:T(8,128)(2,1)S(1)}, u32[]{:S(2)}, u32[]{:S(2)}) collective-permute-start(bf16[520,1024]{1,0:T(8,128)(2,1)S(1)} %get-tuple-element.8), channel_id=1, source_target_pairs={{0,16},{1,17},{2,18},{3,19},{4,20},{5,21},{6,22},{7,23},{8,24},{9,... | collective-permute-start | bytes 3194888 | tf_op jit(solution)/shard_map/ppermute | solution.py:219
  6.2 1.4 %collective-permute-start.10 = (bf16[128,1024]{1,0:T(8,128)(2,1)S(1)}, bf16[128,1024]{1,0:T(8,128)(2,1)}, u32[]{:S(2)}, u32[]{:S(2)}) collective-permute-start(bf16[128,1024]{1,0:T(8,128)(2,1)S(1)} %get-tuple-element.10), channel_id=1, source_target_pairs={{12,0},{28,16},{44,32},{60,48},{76,64},{92,80},{108,96},{124,112},... | collective-permute-start | bytes 786440 | tf_op jit(solution)/shard_map/ppermute | solution.py:219
  7.6 1.4 %collective-permute-start.4 = (bf16[128,1024]{1,0:T(8,128)(2,1)S(1)}, bf16[128,1024]{1,0:T(8,128)(2,1)}, u32[]{:S(2)}, u32[]{:S(2)}) collective-permute-start(bf16[128,1024]{1,0:T(8,128)(2,1)S(1)} %get-tuple-element.10), channel_id=1, source_target_pairs={{7,14},{11,15},{23,30},{27,31},{39,46},{43,47},{55,62},{59,63},{71... | collective-permute-start | bytes 786440 | tf_op jit(solution)/shard_map/ppermute | solution.py:219
  8.9 1.4 %collective-permute-start.6 = (bf16[128,1024]{1,0:T(8,128)(2,1)S(1)}, bf16[128,1024]{1,0:T(8,128)(2,1)}, u32[]{:S(2)}, u32[]{:S(2)}) collective-permute-start(bf16[128,1024]{1,0:T(8,128)(2,1)S(1)} %get-tuple-element.10), channel_id=1, source_target_pairs={{3,15},{19,31},{35,47},{51,63},{67,79},{83,95},{99,111},{115,127},... | collective-permute-start | bytes 786440 | tf_op jit(solution)/shard_map/ppermute | solution.py:219
  10.3 0.0 collective-permute-done.refs_1_
  10.3 8.1 %collective-permute-start.2 = (bf16[392,1024]{1,0:T(8,128)(2,1)S(1)}, bf16[392,1024]{1,0:T(8,128)(2,1)S(1)}, u32[]{:S(2)}, u32[]{:S(2)}) collective-permute-start(bf16[392,1024]{1,0:T(8,128)(2,1)S(1)} %get-tuple-element.9), channel_id=1, source_target_pairs={{1,2},{2,1},{5,6},{6,5},{9,10},{10,9},{13,14},{14,13},{3,4},{4,3},... | collective-permute-start | bytes 2408456 | tf_op jit(solution)/shard_map/ppermute | solution.py:219
  18.4 0.0 copy-start
  18.4 2.8 %copy-done = bf16[3,1024,1024]{2,1,0:T(8,128)(2,1)S(1)} copy-done((bf16[3,1024,1024]{2,1,0:T(8,128)(2,1)S(1)}, bf16[3,1024,1024]{2,1,0:T(8,128)(2,1)}, u32[]{:S(2)}) %copy-start) | copy-done | bytes 6291480
  21.2 0.0 copy-start.1
  21.2 4.3 %shard_map.37.refs_0_ = f32[1,1024,1024]{2,1,0:T(8,128)S(1)} custom-call(s32[1]{0:T(128)S(6)} %sub.3.which_ref, bf16[3,1024,1024]{2,1,0:T(8,128)(2,1)S(1)} %copy-done, bf16[520,1024]{1,0:T(8,128)(2,1)} %collective-permute-done.refs_1_), custom_call_target="tpu_custom_call" | custom-call | flops 4294967296 | bytes 10485760 | tf_op jit(solution)/shard_map/pallas_call | solution.py:145
  25.5 3.4 %collective-permute-done.1.refs_2_ = bf16[520,1024]{1,0:T(8,128)(2,1)S(1)} collective-permute-done((bf16[520,1024]{1,0:T(8,128)(2,1)S(1)}, bf16[520,1024]{1,0:T(8,128)(2,1)S(1)}, u32[]{:S(2)}, u32[]{:S(2)}) %collective-permute-start.1) | collective-permute-done | bytes 1064992 | tf_op jit(solution)/shard_map/ppermute | solution.py:219
  28.9 1.3 %collective-permute-start.8 = (bf16[128,1024]{1,0:T(8,128)(2,1)S(1)}, bf16[128,1024]{1,0:T(8,128)(2,1)S(1)}, u32[]{:S(2)}, u32[]{:S(2)}) collective-permute-start(bf16[128,1024]{1,0:T(8,128)(2,1)S(1)} %get-tuple-element.10), channel_id=1, source_target_pairs={{4,0},{8,1},{20,16},{24,17},{36,32},{40,33},{52,48},{56,49},{68,64... | collective-permute-start | bytes 786440 | tf_op jit(solution)/shard_map/ppermute | solution.py:219
  30.2 0.0 copy-done.1
  30.2 3.0 %shard_map.38.refs_0_ = f32[1,1024,1024]{2,1,0:T(8,128)S(1)} custom-call(s32[1]{0:T(128)} %constant.19.clone.1.which_ref, f32[1,1024,1024]{2,1,0:T(8,128)S(1)} %shard_map.37.refs_0_, bf16[3,1024,1024]{2,1,0:T(8,128)(2,1)S(1)} %copy-done.1, bf16[520,1024]{1,0:T(8,128)(2,1)S(1)} %collective-permute-done.1.refs_2_), custom_call_target="tpu_custom_call" | custom-call | flops 4294967296 | bytes 10485760 | tf_op jit(solution)/shard_map/pallas_call | solution.py:145
  33.2 0.0 collective-permute-done.10
  33.2 8.1 %collective-permute-start.3 = (bf16[128,1024]{1,0:T(8,128)(2,1)S(1)}, bf16[128,1024]{1,0:T(8,128)(2,1)S(1)}, u32[]{:S(2)}, u32[]{:S(2)}) collective-permute-start(bf16[128,1024]{1,0:T(8,128)(2,1)S(1)} %get-tuple-element.10), channel_id=1, source_target_pairs={{1,2},{2,1},{5,6},{6,5},{9,10},{10,9},{13,14},{14,13},{17,18},{18,... | collective-permute-start | bytes 786440 | tf_op jit(solution)/shard_map/ppermute | solution.py:219
  41.3 0.0 collective-permute-done.4
  41.3 0.7 collective-permute-start.11
  42.0 0.0 collective-permute-done.6
  42.0 0.7 collective-permute-start.5
  42.7 0.0 collective-permute-done.8
  42.7 0.7 collective-permute-start.7
  43.4 11.4 %collective-permute-done.2.refs_2_.first_ref = bf16[392,1024]{1,0:T(8,128)(2,1)S(1)} collective-permute-done((bf16[392,1024]{1,0:T(8,128)(2,1)S(1)}, bf16[392,1024]{1,0:T(8,128)(2,1)S(1)}, u32[]{:S(2)}, u32[]{:S(2)}) %collective-permute-start.2) | collective-permute-done | bytes 802848 | tf_op jit(solution)/shard_map/ppermute | solution.py:219
  54.7 12.8 %collective-permute-start.9 = (bf16[128,1024]{1,0:T(8,128)(2,1)S(1)}, bf16[128,1024]{1,0:T(8,128)(2,1)S(1)}, u32[]{:S(2)}, u32[]{:S(2)}) collective-permute-start(bf16[128,1024]{1,0:T(8,128)(2,1)S(1)} %collective-permute-done.8), channel_id=1, source_target_pairs={{0,3},{1,7},{16,19},{17,23},{32,35},{33,39},{48,51},{49,55},{64,67... | collective-permute-start | bytes 786440 | tf_op jit(solution)/shard_map/ppermute | solution.py:219
  67.5 2.4 %shard_map.39.acc_ref = f32[1,1024,1024]{2,1,0:T(8,128)S(1)} custom-call(s32[1]{0:T(128)} %bitcast.which_ref, f32[1,1024,1024]{2,1,0:T(8,128)S(1)} %shard_map.38.refs_0_, bf16[3,1024,1024]{2,1,0:T(8,128)(2,1)S(1)} %copy-done.1, bf16[392,1024]{1,0:T(8,128)(2,1)S(1)} %collective-permute-done.2.refs_2_.first_ref), custom_call_target="tpu_custom_call" | custom-call | flops 3221225472 | bytes 10485760 | tf_op jit(solution)/shard_map/pallas_call | solution.py:145
  69.9 0.0 collective-permute-done.3.refs_0_
  69.9 0.0 collective-permute-done.11.refs_4_
  69.9 0.0 collective-permute-done.5.refs_1_
  70.0 0.0 collective-permute-done.7.refs_2_
  70.0 8.9 %collective-permute-done.9.refs_3_ = bf16[128,1024]{1,0:T(8,128)(2,1)S(1)} collective-permute-done((bf16[128,1024]{1,0:T(8,128)(2,1)S(1)}, bf16[128,1024]{1,0:T(8,128)(2,1)S(1)}, u32[]{:S(2)}, u32[]{:S(2)}) %collective-permute-start.9) | collective-permute-done | bytes 262176 | tf_op jit(solution)/shard_map/ppermute | solution.py:219
  78.9 3.1 %last.1 = f32[1,1024,1024]{2,1,0:T(8,128)} custom-call(s32[1]{0:T(128)} %bitcast.which_ref, f32[1,1024,1024]{2,1,0:T(8,128)S(1)} %shard_map.39.acc_ref, bf16[3,1024,1024]{2,1,0:T(8,128)(2,1)S(1)} %copy-done.1, bf16[392,1024]{1,0:T(8,128)(2,1)S(1)} %collective-permute-done.2.refs_2_.first_ref, bf16[128,1024]{1,0:T(8,128)(2,1)S(1)} %collective-permute-done.3.refs_0_, ...), custom_call_target="tpu_custom_call" | custom-call | flops 1073741824 | bytes 10485760 | tf_op jit(solution)/shard_map/last/pallas_call | solution.py:199
Async XLA Ops:
  2.2 8.1 %collective-permute-start = (bf16[520,1024]{1,0:T(8,128)(2,1)S(1)}, bf16[520,1024]{1,0:T(8,128)(2,1)}, u32[]{:S(2)}, u32[]{:S(2)}) collective-permute-start(bf16[520,1024]{1,0:T(8,128)(2,1)S(1)} %get-tuple-element.8), channel_id=1, source_target_pairs={{0,1},{1,0},{2,3},{3,2},{4,5},{5,4},{6,7},{7,6},{8,9},{9,8},{10,11... | collective-permute-start | bytes 3194888 | tf_op jit(solution)/shard_map/ppermute | solution.py:219
  2.9 26.0 %collective-permute-start.1 = (bf16[520,1024]{1,0:T(8,128)(2,1)S(1)}, bf16[520,1024]{1,0:T(8,128)(2,1)S(1)}, u32[]{:S(2)}, u32[]{:S(2)}) collective-permute-start(bf16[520,1024]{1,0:T(8,128)(2,1)S(1)} %get-tuple-element.8), channel_id=1, source_target_pairs={{0,16},{1,17},{2,18},{3,19},{4,20},{5,21},{6,22},{7,23},{8,24},{9,... | collective-permute-start | bytes 3194888 | tf_op jit(solution)/shard_map/ppermute | solution.py:219
  6.2 27.0 %collective-permute-start.10 = (bf16[128,1024]{1,0:T(8,128)(2,1)S(1)}, bf16[128,1024]{1,0:T(8,128)(2,1)}, u32[]{:S(2)}, u32[]{:S(2)}) collective-permute-start(bf16[128,1024]{1,0:T(8,128)(2,1)S(1)} %get-tuple-element.10), channel_id=1, source_target_pairs={{12,0},{28,16},{44,32},{60,48},{76,64},{92,80},{108,96},{124,112},... | collective-permute-start | bytes 786440 | tf_op jit(solution)/shard_map/ppermute | solution.py:219
  7.6 33.7 %collective-permute-start.4 = (bf16[128,1024]{1,0:T(8,128)(2,1)S(1)}, bf16[128,1024]{1,0:T(8,128)(2,1)}, u32[]{:S(2)}, u32[]{:S(2)}) collective-permute-start(bf16[128,1024]{1,0:T(8,128)(2,1)S(1)} %get-tuple-element.10), channel_id=1, source_target_pairs={{7,14},{11,15},{23,30},{27,31},{39,46},{43,47},{55,62},{59,63},{71... | collective-permute-start | bytes 786440 | tf_op jit(solution)/shard_map/ppermute | solution.py:219
  8.9 33.1 %collective-permute-start.6 = (bf16[128,1024]{1,0:T(8,128)(2,1)S(1)}, bf16[128,1024]{1,0:T(8,128)(2,1)}, u32[]{:S(2)}, u32[]{:S(2)}) collective-permute-start(bf16[128,1024]{1,0:T(8,128)(2,1)S(1)} %get-tuple-element.10), channel_id=1, source_target_pairs={{3,15},{19,31},{35,47},{51,63},{67,79},{83,95},{99,111},{115,127},... | collective-permute-start | bytes 786440 | tf_op jit(solution)/shard_map/ppermute | solution.py:219
  10.3 44.4 %collective-permute-start.2 = (bf16[392,1024]{1,0:T(8,128)(2,1)S(1)}, bf16[392,1024]{1,0:T(8,128)(2,1)S(1)}, u32[]{:S(2)}, u32[]{:S(2)}) collective-permute-start(bf16[392,1024]{1,0:T(8,128)(2,1)S(1)} %get-tuple-element.9), channel_id=1, source_target_pairs={{1,2},{2,1},{5,6},{6,5},{9,10},{10,9},{13,14},{14,13},{3,4},{4,3},... | collective-permute-start | bytes 2408456 | tf_op jit(solution)/shard_map/ppermute | solution.py:219
  18.4 2.8 %copy-start = (bf16[3,1024,1024]{2,1,0:T(8,128)(2,1)S(1)}, bf16[3,1024,1024]{2,1,0:T(8,128)(2,1)}, u32[]{:S(2)}) copy-start(bf16[3,1024,1024]{2,1,0:T(8,128)(2,1)} %c_ref.1) | copy-start | bytes 18874372
  21.2 9.0 %copy-start.1 = (bf16[3,1024,1024]{2,1,0:T(8,128)(2,1)S(1)}, bf16[3,1024,1024]{2,1,0:T(8,128)(2,1)}, u32[]{:S(2)}) copy-start(bf16[3,1024,1024]{2,1,0:T(8,128)(2,1)} %c_ref.1) | copy-start | bytes 18874372
  28.9 13.8 %collective-permute-start.8 = (bf16[128,1024]{1,0:T(8,128)(2,1)S(1)}, bf16[128,1024]{1,0:T(8,128)(2,1)S(1)}, u32[]{:S(2)}, u32[]{:S(2)}) collective-permute-start(bf16[128,1024]{1,0:T(8,128)(2,1)S(1)} %get-tuple-element.10), channel_id=1, source_target_pairs={{4,0},{8,1},{20,16},{24,17},{36,32},{40,33},{52,48},{56,49},{68,64... | collective-permute-start | bytes 786440 | tf_op jit(solution)/shard_map/ppermute | solution.py:219
  33.2 36.7 %collective-permute-start.3 = (bf16[128,1024]{1,0:T(8,128)(2,1)S(1)}, bf16[128,1024]{1,0:T(8,128)(2,1)S(1)}, u32[]{:S(2)}, u32[]{:S(2)}) collective-permute-start(bf16[128,1024]{1,0:T(8,128)(2,1)S(1)} %get-tuple-element.10), channel_id=1, source_target_pairs={{1,2},{2,1},{5,6},{6,5},{9,10},{10,9},{13,14},{14,13},{17,18},{18,... | collective-permute-start | bytes 786440 | tf_op jit(solution)/shard_map/ppermute | solution.py:219
  41.3 28.6 %collective-permute-start.11 = (bf16[128,1024]{1,0:T(8,128)(2,1)}, bf16[128,1024]{1,0:T(8,128)(2,1)S(1)}, u32[]{:S(2)}, u32[]{:S(2)}) collective-permute-start(bf16[128,1024]{1,0:T(8,128)(2,1)} %collective-permute-done.10), channel_id=1, source_target_pairs={{0,11},{16,27},{32,43},{48,59},{64,75},{80,91},{96,107},{112,123},... | collective-permute-start | bytes 786440 | tf_op jit(solution)/shard_map/ppermute | solution.py:219
  42.0 27.9 %collective-permute-start.5 = (bf16[128,1024]{1,0:T(8,128)(2,1)}, bf16[128,1024]{1,0:T(8,128)(2,1)S(1)}, u32[]{:S(2)}, u32[]{:S(2)}) collective-permute-start(bf16[128,1024]{1,0:T(8,128)(2,1)} %collective-permute-done.4), channel_id=1, source_target_pairs={{14,8},{15,12},{30,24},{31,28},{46,40},{47,44},{62,56},{63,60},{78... | collective-permute-start | bytes 786440 | tf_op jit(solution)/shard_map/ppermute | solution.py:219
  42.7 27.3 %collective-permute-start.7 = (bf16[128,1024]{1,0:T(8,128)(2,1)}, bf16[128,1024]{1,0:T(8,128)(2,1)S(1)}, u32[]{:S(2)}, u32[]{:S(2)}) collective-permute-start(bf16[128,1024]{1,0:T(8,128)(2,1)} %collective-permute-done.6), channel_id=1, source_target_pairs={{15,4},{31,20},{47,36},{63,52},{79,68},{95,84},{111,100},{127,116}... | collective-permute-start | bytes 786440 | tf_op jit(solution)/shard_map/ppermute | solution.py:219
  54.7 24.2 %collective-permute-start.9 = (bf16[128,1024]{1,0:T(8,128)(2,1)S(1)}, bf16[128,1024]{1,0:T(8,128)(2,1)S(1)}, u32[]{:S(2)}, u32[]{:S(2)}) collective-permute-start(bf16[128,1024]{1,0:T(8,128)(2,1)S(1)} %collective-permute-done.8), channel_id=1, source_target_pairs={{0,3},{1,7},{16,19},{17,23},{32,35},{33,39},{48,51},{49,55},{64,67... | collective-permute-start | bytes 786440 | tf_op jit(solution)/shard_map/ppermute | solution.py:219

commit v3 on v2

--- a/solution.py
+++ b/solution.py
@@ -69,7 +69,7 @@
         ],
         out_specs=(pl.BlockSpec(memory_space=pltpu.VMEM),) * 3,
         scratch_shapes=[pltpu.VMEM((width, width), jnp.bfloat16), pltpu.SemaphoreType.DMA((width // B,))],
-        compiler_params=pltpu.CompilerParams(vmem_limit_bytes=60 << 20),
+        compiler_params=pltpu.CompilerParams(vmem_limit_bytes=57 << 20),
         cost_estimate=pl.CostEstimate(flops=4 * width * width, bytes_accessed=3 * width * width, transcendentals=0),
         name="pack",
     )(sep_sizes, factor_inv)
@@ -101,10 +101,14 @@
         )
 
 
+def gathered(refs, rows):
+    return sum((ref[rows, :] for ref in refs[1:]), refs[0][rows, :])
+
+
 def slot_kernel(units, has_acc, whole, which_ref, *refs):
     if has_acc:
         acc_ref, *refs = refs
-    c_ref, part_ref, out_ref, g, x = refs
+    c_ref, *part_refs, out_ref, g, x = refs
     which = which_ref[0]
     n = c_ref.shape[1] // B
     panels = sorted([u for u in units] + [n - 1 - u for u in units])
@@ -112,10 +116,10 @@
     for k in range(0, len(panels), 2):
         lo, hi = panels[k], panels[k + 1]
         g[k * B:(k + 1) * B, (lo + 1) * B:(hi + 1) * B] = jnp.zeros((B, (hi - lo) * B), jnp.bfloat16)
-    diag = part_ref[0:1, :]
+    diag = gathered(part_refs, slice(0, 1))
     for u in units:
         at = EXTRA + B * u
-        place(g, (where[u], where[n - 1 - u]), part_ref[at:at + B, :], u, diag, n)
+        place(g, (where[u], where[n - 1 - u]), gathered(part_refs, slice(at, at + B)), u, diag, n)
     wide = 2 * B
     depths = [(panels[k + 1] + 1) * B for k in range(0, len(panels), 2)]
     for b in range(n // 2):
@@ -138,10 +142,10 @@
                 out_ref[0, cols, k * wide:(k + 1) * wide] = part[(k - b) * wide:(k - b + 1) * wide].T
 
 
-def update(which, coupling, part, units, acc, whole=False):
+def update(which, coupling, parts, units, acc, whole=False):
     width = coupling.shape[1]
     rows = 2 * B * len(units)
-    ins = ([acc] if acc is not None else []) + [coupling, part]
+    ins = ([acc] if acc is not None else []) + [coupling, *parts]
     return pl.pallas_call(
         functools.partial(slot_kernel, units, acc is not None, whole),
         out_shape=jax.ShapeDtypeStruct((1, width, width), jnp.float32),
@@ -151,7 +155,7 @@
             pltpu.VMEM((rows, width), jnp.bfloat16),
             pltpu.VMEM((rows, width), jnp.bfloat16),
         ],
-        compiler_params=pltpu.CompilerParams(vmem_limit_bytes=24 << 20),
+        compiler_params=pltpu.CompilerParams(vmem_limit_bytes=12 << 20),
         cost_estimate=pl.CostEstimate(
             flops=4 * rows * width * width, bytes_accessed=10 * width * width, transcendentals=0
         ),
@@ -159,7 +163,7 @@
 
 
 def last_kernel(which_ref, acc_ref, c_ref, first_ref, *refs):
-    last_refs, (out_ref, g, x, sums, sems) = refs[:-5], refs[-5:]
+    last_refs, (out_ref, g, x, sums, sems) = refs[:3], refs[-5:]
     which = which_ref[0]
     n = c_ref.shape[1] // B
     panels = sorted([u for u in UNITS_LAST] + [n - 1 - u for u in UNITS_LAST])
@@ -169,7 +173,7 @@
         g[k * B:(k + 1) * B, (lo + 1) * B:(hi + 1) * B] = jnp.zeros((B, (hi - lo) * B), jnp.bfloat16)
     for u in UNITS_LAST:
         at = B * UNITS_LAST.index(u)
-        unit = sum((ref[at:at + B, :] for ref in last_refs[1:]), last_refs[0][at:at + B, :])
+        unit = gathered(last_refs, slice(at, at + B))
         place(g, (where[u], where[n - 1 - u]), unit, u, first_ref[0:1, :], n)
     blocks = 4
     wide = n * B // blocks
@@ -207,7 +211,7 @@
             pltpu.VMEM((width, width), jnp.float32),
             pltpu.SemaphoreType.DMA((4,)),
         ],
-        compiler_params=pltpu.CompilerParams(vmem_limit_bytes=16 << 20),
+        compiler_params=pltpu.CompilerParams(vmem_limit_bytes=10 << 20),
         cost_estimate=pl.CostEstimate(
             flops=4 * rows * width * width, bytes_accessed=10 * width * width, transcendentals=0
         ),
@@ -220,8 +224,8 @@
 
 
 def routes(n_lo, n_y, n_z):
-    big, small, near, up = [], [], [], []
-    aside, beside, rising, falling = (([], []) for _ in range(4))
+    big, small, near, up, late = [], [], [], [], []
+    aside, onward = ([], []), ([], [])
     columns = n_z // 4
     for lo in range(n_lo):
         for y in range(n_y):
@@ -229,7 +233,9 @@
             for k in range(0, n_z, 2):
                 near += [(at(k), at(k + 1)), (at(k + 1), at(k))]
             if y + 1 < n_y:
-                up += [(at(k), at(k) + n_z) for k in range(n_z)]
+                for k in range(n_z):
+                    relays = k % 2 == 0 if k % 4 < 2 else k == n_z - 1
+                    (late if relays else up).append((at(k), at(k) + n_z))
             for x in range(columns):
                 for pair in ((4 * x + 1, 4 * x + 2), (4 * x + 2, 4 * x + 1)):
                     big.append(tuple(map(at, pair)))
@@ -239,30 +245,27 @@
                 right, left = 4 * x + 3, 4 * x + 4
                 turn, side = divmod(columns - 2 - x, 2)
                 back, other = divmod(x, 2)
-                for source, target, relay, first, onward, which in (
-                    (right, left, end + 3 - side, aside, rising, turn),
-                    (left, right, other, beside, falling, back),
+                for source, target, relay, which in (
+                    (right, left, end + 3 - side, turn),
+                    (left, right, other, back),
                 ):
                     big.append((at(source), at(target)))
-                    first[which].append((at(source), at(relay)))
+                    aside[which].append((at(source), at(relay)))
                     onward[which].append((at(relay), at(target)))
-    return big, small, aside, rising, beside, falling, near, up
+    return big, small, aside, onward, near, up, late
 
 
 def on_device(factor_inv, sep_sizes, coupling):
     first, last, full = packed(factor_inv, sep_sizes)
-    big, small, aside, rising, beside, falling, near_pairs, up = routes(*(lax.axis_size(a) for a in ("gx", "gy", "gz")))
+    big, small, aside, onward, near_pairs, up, late = routes(*(lax.axis_size(a) for a in ("gx", "gy", "gz")))
     far_first = moved(first, big)
     side_a = moved(last, aside[0])
     side_b = moved(last, aside[1])
     far_last = moved(last, small)
-    rising_a = moved(side_a, rising[0])
-    rising_b = moved(side_b, rising[1])
     below_y = moved(full, up)
-    side_c = moved(last, beside[0])
-    side_d = moved(last, beside[1])
-    falling_a = moved(side_c, falling[0])
-    falling_b = moved(side_d, falling[1])
+    on_a = moved(side_a, onward[0])
+    on_b = moved(side_b, onward[1])
+    late_y = moved(full, late)
     near = moved(full, near_pairs)
 
     odd = lax.axis_index("gz") % 2
@@ -270,10 +273,10 @@
     near_slot = 1 - far_slot
     y_slot = jnp.full((1,), 2, jnp.int32)
     every = UNITS_FIRST + UNITS_LAST
-    total = update(near_slot, coupling, near, every, None)
-    total = update(y_slot, coupling, below_y, every, total)
-    total = update(far_slot, coupling, far_first, UNITS_FIRST, total, whole=True)
-    return last_update(far_slot, coupling, (far_first, far_last, rising_a, rising_b, falling_a, falling_b), total)
+    total = update(near_slot, coupling, (near,), every, None)
+    total = update(y_slot, coupling, (below_y, late_y), every, total)
+    total = update(far_slot, coupling, (far_first,), UNITS_FIRST, total, whole=True)
+    return last_update(far_slot, coupling, (far_first, *(far_last, on_a, on_b) * 4), total)
 
 
 def solution(mesh):

time: 82.3 us -> 68.9 us (0.84)
  the two profiles are of different devices: /device:TPU:33 before, /device:TPU:2 now
where the time goes in v3:
time: 68.9 us; the launch traced here: 68.6 us
  waiting for transfers between devices  27.9 us (40%)
  starting transfers between devices  22.2 us (32%)
  Pallas kernels  14.1 us (20%)
  local copies, waits for them, and re-layouts  3.66 us (5%)
  between operations  0.8 us (1%)
    ppermute x9, waiting for transfers between devices, moved(): return lax.ppermute(block, ('gx', 'gy', 'gz'), pairs)  27.9 us
    ppermute x9, starting transfers between devices, moved(): return lax.ppermute(block, ('gx', 'gy', 'gz'), pairs)  22.2 us
    pallas_call x3, Pallas kernels, update(): pl.pallas_call(functools.partial(slot_kernel, units, acc is not None, who...  9.58 us
    unnamed x6, local copies, waits for them, and re-layouts  3.66 us
    pallas_call x1, Pallas kernels, last_update(): pl.pallas_call(last_kernel, out_shape=jax.ShapeDtypeStruct((1, width, wid...  3 us
    pallas_call x1, Pallas kernels, packed(): pl.pallas_call(pack_kernel, out_shape=tuple((pltpu.VMEM((rows, width), jn...  1.49 us
  transfers between devices with their start and end apart: 9, of which 2 were waited for; matrix products, arithmetic and copies ran while one was open for 0% of the time, Pallas kernels for 14%

profile of v3, /device:TPU:2, one launch (start us, length us, event | category | flops | bytes accessed | tf_op | source)
XLA Modules:
  0.0 68.6 jit_solution(4470863285653810153)
XLA Ops:
  0.7 1.5 %pack.1 = (bf16[392,1024]{1,0:T(8,128)(2,1)S(1)}, bf16[128,1024]{1,0:T(8,128)(2,1)S(1)}, bf16[520,1024]{1,0:T(8,128)(2,1)S(1)}) custom-call(s32[1,1,1]{2,1,0:T(1,128)S(6)} %copy.4.size_ref, bf16[1,1024,1024]{2,1,0:T(8,128)(2,1)} %f_ref.1), custom_call_target="tpu_custom_call" | custom-call | flops 4194304 | bytes 3145728 | tf_op jit(solution)/shard_map/pack/pallas_call | solution.py:63
  2.2 0.0 copy-start.2
  2.2 0.9 %copy-done.2 = bf16[392,1024]{1,0:T(8,128)(2,1)} copy-done((bf16[392,1024]{1,0:T(8,128)(2,1)}, bf16[392,1024]{1,0:T(8,128)(2,1)S(1)}, u32[]{:S(2)}) %copy-start.2) | copy-done | bytes 802840
  3.0 0.0 collective-permute-start
  3.0 0.7 %collective-permute-start.1 = (bf16[520,1024]{1,0:T(8,128)(2,1)S(1)}, bf16[520,1024]{1,0:T(8,128)(2,1)S(1)}, u32[]{:S(2)}, u32[]{:S(2)}) collective-permute-start(bf16[520,1024]{1,0:T(8,128)(2,1)S(1)} %get-tuple-element.8), channel_id=1, source_target_pairs={{1,17},{2,18},{3,19},{5,21},{6,22},{7,23},{9,25},{10,26},{11,27},{... | collective-permute-start | bytes 3194888 | tf_op jit(solution)/shard_map/ppermute | solution.py:223
  3.8 3.5 %collective-permute-start.2 = (bf16[520,1024]{1,0:T(8,128)(2,1)S(1)}, bf16[520,1024]{1,0:T(8,128)(2,1)S(1)}, u32[]{:S(2)}, u32[]{:S(2)}) collective-permute-start(bf16[520,1024]{1,0:T(8,128)(2,1)S(1)} %get-tuple-element.8), channel_id=1, source_target_pairs={{0,16},{4,20},{8,24},{12,28},{15,31},{16,32},{20,36},{24,40},{28,4... | collective-permute-start | bytes 3194888 | tf_op jit(solution)/shard_map/ppermute | solution.py:223
  7.3 3.2 %collective-permute-start.5 = (bf16[128,1024]{1,0:T(8,128)(2,1)S(1)}, bf16[128,1024]{1,0:T(8,128)(2,1)}, u32[]{:S(2)}, u32[]{:S(2)}) collective-permute-start(bf16[128,1024]{1,0:T(8,128)(2,1)S(1)} %get-tuple-element.10), channel_id=1, source_target_pairs={{4,0},{7,14},{8,1},{11,15},{20,16},{23,30},{24,17},{27,31},{36,32}... | collective-permute-start | bytes 786440 | tf_op jit(solution)/shard_map/ppermute | solution.py:223
  10.5 1.4 %collective-permute-start.7 = (bf16[128,1024]{1,0:T(8,128)(2,1)S(1)}, bf16[128,1024]{1,0:T(8,128)(2,1)}, u32[]{:S(2)}, u32[]{:S(2)}) collective-permute-start(bf16[128,1024]{1,0:T(8,128)(2,1)S(1)} %get-tuple-element.10), channel_id=1, source_target_pairs={{3,15},{12,0},{19,31},{28,16},{35,47},{44,32},{51,63},{60,48},{67,... | collective-permute-start | bytes 786440 | tf_op jit(solution)/shard_map/ppermute | solution.py:223
  11.8 0.0 collective-permute-done.refs_1_
  11.8 10.8 %collective-permute-start.3 = (bf16[392,1024]{1,0:T(8,128)(2,1)}, bf16[392,1024]{1,0:T(8,128)(2,1)S(1)}, u32[]{:S(2)}, u32[]{:S(2)}) collective-permute-start(bf16[392,1024]{1,0:T(8,128)(2,1)} %copy-done.2), channel_id=1, source_target_pairs={{1,2},{2,1},{5,6},{6,5},{9,10},{10,9},{13,14},{14,13},{3,4},{4,3},... | collective-permute-start | bytes 2408456 | tf_op jit(solution)/shard_map/ppermute | solution.py:223
  22.6 0.0 copy-start
  22.6 2.8 %copy-done = bf16[3,1024,1024]{2,1,0:T(8,128)(2,1)S(1)} copy-done((bf16[3,1024,1024]{2,1,0:T(8,128)(2,1)S(1)}, bf16[3,1024,1024]{2,1,0:T(8,128)(2,1)}, u32[]{:S(2)}) %copy-start) | copy-done | bytes 6291480
  25.4 0.0 copy-start.1
  25.4 4.3 %shard_map.37.refs_0_ = f32[1,1024,1024]{2,1,0:T(8,128)S(1)} custom-call(s32[1]{0:T(128)S(6)} %sub.3.which_ref, bf16[3,1024,1024]{2,1,0:T(8,128)(2,1)S(1)} %copy-done, bf16[520,1024]{1,0:T(8,128)(2,1)} %collective-permute-done.refs_1_), custom_call_target="tpu_custom_call" | custom-call | flops 4294967296 | bytes 10485760 | tf_op jit(solution)/shard_map/pallas_call | solution.py:149
  29.7 0.0 collective-permute-done.5
  29.7 0.7 collective-permute-start.4
  30.4 0.0 collective-permute-done.7
  30.4 0.7 collective-permute-start.6
  31.1 0.0 collective-permute-done.1.refs_2_
  31.1 1.3 %collective-permute-start.8 = (bf16[128,1024]{1,0:T(8,128)(2,1)}, bf16[128,1024]{1,0:T(8,128)(2,1)S(1)}, u32[]{:S(2)}, u32[]{:S(2)}) collective-permute-start(bf16[128,1024]{1,0:T(8,128)(2,1)} %collective-permute-done.7), channel_id=1, source_target_pairs={{15,4},{0,11},{31,20},{16,27},{47,36},{32,43},{63,52},{48,59},{79,... | collective-permute-start | bytes 786440 | tf_op jit(solution)/shard_map/ppermute | solution.py:223
  32.4 0.0 collective-permute-done.2.refs_3_
  32.4 0.0 copy-done.1
  32.4 2.9 %shard_map.38.refs_0_ = f32[1,1024,1024]{2,1,0:T(8,128)S(1)} custom-call(s32[1]{0:T(128)} %constant.19.clone.1.which_ref, f32[1,1024,1024]{2,1,0:T(8,128)S(1)} %shard_map.37.refs_0_, bf16[3,1024,1024]{2,1,0:T(8,128)(2,1)S(1)} %copy-done.1, bf16[520,1024]{1,0:T(8,128)(2,1)S(1)} %collective-permute-done.1.refs_2_, ...), custom_call_target="tpu_custom_call" | custom-call | flops 4294967296 | bytes 10485760 | tf_op jit(solution)/shard_map/pallas_call | solution.py:149
  35.4 11.5 %collective-permute-done.3.refs_2_.first_ref = bf16[392,1024]{1,0:T(8,128)(2,1)S(1)} collective-permute-done((bf16[392,1024]{1,0:T(8,128)(2,1)}, bf16[392,1024]{1,0:T(8,128)(2,1)S(1)}, u32[]{:S(2)}, u32[]{:S(2)}) %collective-permute-start.3) | collective-permute-done | bytes 802848 | tf_op jit(solution)/shard_map/ppermute | solution.py:223
  46.9 2.4 %shard_map.39.acc_ref = f32[1,1024,1024]{2,1,0:T(8,128)S(1)} custom-call(s32[1]{0:T(128)} %bitcast.which_ref, f32[1,1024,1024]{2,1,0:T(8,128)S(1)} %shard_map.38.refs_0_, bf16[3,1024,1024]{2,1,0:T(8,128)(2,1)S(1)} %copy-done.1, bf16[392,1024]{1,0:T(8,128)(2,1)S(1)} %collective-permute-done.3.refs_2_.first_ref), custom_call_target="tpu_custom_call" | custom-call | flops 3221225472 | bytes 10485760 | tf_op jit(solution)/shard_map/pallas_call | solution.py:149
  49.3 0.0 collective-permute-done.4.refs_0_.refs_3_.refs_6_.refs_9_
  49.3 0.0 collective-permute-done.6.refs_1_.refs_4_.refs_7_.refs_10_
  49.3 16.3 %collective-permute-done.8.refs_2_.refs_5_.refs_8_.refs_11_ = bf16[128,1024]{1,0:T(8,128)(2,1)S(1)} collective-permute-done((bf16[128,1024]{1,0:T(8,128)(2,1)}, bf16[128,1024]{1,0:T(8,128)(2,1)S(1)}, u32[]{:S(2)}, u32[]{:S(2)}) %collective-permute-start.8) | collective-permute-done | bytes 262176 | tf_op jit(solution)/shard_map/ppermute | solution.py:223
  65.6 3.0 %last.1 = f32[1,1024,1024]{2,1,0:T(8,128)} custom-call(s32[1]{0:T(128)} %bitcast.which_ref, f32[1,1024,1024]{2,1,0:T(8,128)S(1)} %shard_map.39.acc_ref, bf16[3,1024,1024]{2,1,0:T(8,128)(2,1)S(1)} %copy-done.1, bf16[392,1024]{1,0:T(8,128)(2,1)S(1)} %collective-permute-done.3.refs_2_.first_ref, ...), custom_call_target="tpu_custom_call" | custom-call | flops 1073741824 | bytes 10485760 | tf_op jit(solution)/shard_map/last/pallas_call | solution.py:203
Async XLA Ops:
  2.2 0.9 %copy-start.2 = (bf16[392,1024]{1,0:T(8,128)(2,1)}, bf16[392,1024]{1,0:T(8,128)(2,1)S(1)}, u32[]{:S(2)}) copy-start(bf16[392,1024]{1,0:T(8,128)(2,1)S(1)} %get-tuple-element.9) | copy-start | bytes 2408452
  3.0 8.8 %collective-permute-start = (bf16[520,1024]{1,0:T(8,128)(2,1)S(1)}, bf16[520,1024]{1,0:T(8,128)(2,1)}, u32[]{:S(2)}, u32[]{:S(2)}) collective-permute-start(bf16[520,1024]{1,0:T(8,128)(2,1)S(1)} %get-tuple-element.8), channel_id=1, source_target_pairs={{0,1},{1,0},{2,3},{3,2},{4,5},{5,4},{6,7},{7,6},{8,9},{9,8},{10,11... | collective-permute-start | bytes 3194888 | tf_op jit(solution)/shard_map/ppermute | solution.py:223
  3.0 28.1 %collective-permute-start.1 = (bf16[520,1024]{1,0:T(8,128)(2,1)S(1)}, bf16[520,1024]{1,0:T(8,128)(2,1)S(1)}, u32[]{:S(2)}, u32[]{:S(2)}) collective-permute-start(bf16[520,1024]{1,0:T(8,128)(2,1)S(1)} %get-tuple-element.8), channel_id=1, source_target_pairs={{1,17},{2,18},{3,19},{5,21},{6,22},{7,23},{9,25},{10,26},{11,27},{... | collective-permute-start | bytes 3194888 | tf_op jit(solution)/shard_map/ppermute | solution.py:223
  3.8 28.6 %collective-permute-start.2 = (bf16[520,1024]{1,0:T(8,128)(2,1)S(1)}, bf16[520,1024]{1,0:T(8,128)(2,1)S(1)}, u32[]{:S(2)}, u32[]{:S(2)}) collective-permute-start(bf16[520,1024]{1,0:T(8,128)(2,1)S(1)} %get-tuple-element.8), channel_id=1, source_target_pairs={{0,16},{4,20},{8,24},{12,28},{15,31},{16,32},{20,36},{24,40},{28,4... | collective-permute-start | bytes 3194888 | tf_op jit(solution)/shard_map/ppermute | solution.py:223
  7.3 22.4 %collective-permute-start.5 = (bf16[128,1024]{1,0:T(8,128)(2,1)S(1)}, bf16[128,1024]{1,0:T(8,128)(2,1)}, u32[]{:S(2)}, u32[]{:S(2)}) collective-permute-start(bf16[128,1024]{1,0:T(8,128)(2,1)S(1)} %get-tuple-element.10), channel_id=1, source_target_pairs={{4,0},{7,14},{8,1},{11,15},{20,16},{23,30},{24,17},{27,31},{36,32}... | collective-permute-start | bytes 786440 | tf_op jit(solution)/shard_map/ppermute | solution.py:223
  10.5 19.9 %collective-permute-start.7 = (bf16[128,1024]{1,0:T(8,128)(2,1)S(1)}, bf16[128,1024]{1,0:T(8,128)(2,1)}, u32[]{:S(2)}, u32[]{:S(2)}) collective-permute-start(bf16[128,1024]{1,0:T(8,128)(2,1)S(1)} %get-tuple-element.10), channel_id=1, source_target_pairs={{3,15},{12,0},{19,31},{28,16},{35,47},{44,32},{51,63},{60,48},{67,... | collective-permute-start | bytes 786440 | tf_op jit(solution)/shard_map/ppermute | solution.py:223
  11.8 35.1 %collective-permute-start.3 = (bf16[392,1024]{1,0:T(8,128)(2,1)}, bf16[392,1024]{1,0:T(8,128)(2,1)S(1)}, u32[]{:S(2)}, u32[]{:S(2)}) collective-permute-start(bf16[392,1024]{1,0:T(8,128)(2,1)} %copy-done.2), channel_id=1, source_target_pairs={{1,2},{2,1},{5,6},{6,5},{9,10},{10,9},{13,14},{14,13},{3,4},{4,3},... | collective-permute-start | bytes 2408456 | tf_op jit(solution)/shard_map/ppermute | solution.py:223
  22.6 2.8 %copy-start = (bf16[3,1024,1024]{2,1,0:T(8,128)(2,1)S(1)}, bf16[3,1024,1024]{2,1,0:T(8,128)(2,1)}, u32[]{:S(2)}) copy-start(bf16[3,1024,1024]{2,1,0:T(8,128)(2,1)} %c_ref.1) | copy-start | bytes 18874372
  25.4 7.0 %copy-start.1 = (bf16[3,1024,1024]{2,1,0:T(8,128)(2,1)S(1)}, bf16[3,1024,1024]{2,1,0:T(8,128)(2,1)}, u32[]{:S(2)}) copy-start(bf16[3,1024,1024]{2,1,0:T(8,128)(2,1)} %c_ref.1) | copy-start | bytes 18874372
  29.7 19.6 %collective-permute-start.4 = (bf16[128,1024]{1,0:T(8,128)(2,1)S(1)}, bf16[128,1024]{1,0:T(8,128)(2,1)S(1)}, u32[]{:S(2)}, u32[]{:S(2)}) collective-permute-start(bf16[128,1024]{1,0:T(8,128)(2,1)S(1)} %get-tuple-element.10), channel_id=1, source_target_pairs={{1,2},{2,1},{5,6},{6,5},{9,10},{10,9},{13,14},{14,13},{17,18},{18,... | collective-permute-start | bytes 786440 | tf_op jit(solution)/shard_map/ppermute | solution.py:223
  30.4 18.9 %collective-permute-start.6 = (bf16[128,1024]{1,0:T(8,128)(2,1)}, bf16[128,1024]{1,0:T(8,128)(2,1)S(1)}, u32[]{:S(2)}, u32[]{:S(2)}) collective-permute-start(bf16[128,1024]{1,0:T(8,128)(2,1)} %collective-permute-done.5), channel_id=1, source_target_pairs={{0,3},{14,8},{1,7},{15,12},{16,19},{30,24},{17,23},{31,28},{32,35}... | collective-permute-start | bytes 786440 | tf_op jit(solution)/shard_map/ppermute | solution.py:223
  31.1 34.5 %collective-permute-start.8 = (bf16[128,1024]{1,0:T(8,128)(2,1)}, bf16[128,1024]{1,0:T(8,128)(2,1)S(1)}, u32[]{:S(2)}, u32[]{:S(2)}) collective-permute-start(bf16[128,1024]{1,0:T(8,128)(2,1)} %collective-permute-done.7), channel_id=1, source_target_pairs={{15,4},{0,11},{31,20},{16,27},{47,36},{32,43},{63,52},{48,59},{79,... | collective-permute-start | bytes 786440 | tf_op jit(solution)/shard_map/ppermute | solution.py:223

commit v4 on v3

--- a/solution.py
+++ b/solution.py
@@ -17,7 +17,6 @@
 def pack_kernel(size_ref, f_ref, first_ref, last_ref, full_ref, held, sems):
     count = size_ref[0, 0, 0]
     n = f_ref.shape[1] // B
-    width = n * B
     i = lax.broadcasted_iota(jnp.int32, (B, B), 0)
     j = lax.broadcasted_iota(jnp.int32, (B, B), 1)
     row = lax.broadcasted_iota(jnp.int32, (B, 1), 0)
@@ -32,7 +31,7 @@
     diags = []
     for u in range(n // 2):
         big = n - 1 - u
-        out, at = (first_ref, EXTRA + B * UNITS_FIRST.index(u)) if u in UNITS_FIRST else (last_ref, B * UNITS_LAST.index(u))
+        out, at = (first_ref, UNITS_FIRST.index(u)) if u in UNITS_FIRST else (last_ref, UNITS_LAST.index(u))
         copy(big).wait()
         copy(u).wait()
         keep_big = (row + big * B) < count
@@ -45,31 +44,31 @@
         d_small = rows_small[:, u * B:(u + 1) * B].astype(jnp.float32)
         square = jnp.where(i >= j, d_small, d_big.T).astype(jnp.bfloat16)
         diags.append(jnp.sum(jnp.where(i == j, d_big, 0.0), axis=0, keepdims=True))
-        for ref, to in ((out, at), (full_ref, EXTRA + B * u)):
-            ref[to:to + B, 0:big * B] = rows_big[:, 0:big * B]
-            ref[to:to + B, big * B:(big + 1) * B] = square
-            if u:
-                ref[to:to + B, (big + 1) * B:width] = rows_small[:, 0:u * B]
-    line = jnp.concatenate(diags + [jnp.zeros((1, width - B * len(diags)), jnp.float32)], axis=1)
-    line = jnp.broadcast_to(line, (EXTRA, width)).astype(jnp.bfloat16)
-    first_ref[0:EXTRA, :] = line
-    full_ref[0:EXTRA, :] = line
+        blocks = [rows_big[:, c * B:(c + 1) * B] for c in range(big)] + [square]
+        blocks += [rows_small[:, c * B:(c + 1) * B] for c in range(u)]
+        for ref, to in ((out, at * n), (full_ref, u * n)):
+            for c, block in enumerate(blocks):
+                ref[(to + c) * B:(to + c + 1) * B, :] = block
+    lines = jnp.concatenate(diags + [jnp.zeros((EXTRA - len(diags), B), jnp.float32)], axis=0)
+    lines = lines.astype(jnp.bfloat16)
+    first_ref[first_ref.shape[0] - EXTRA:, :] = lines
+    full_ref[full_ref.shape[0] - EXTRA:, :] = lines
 
 
 def packed(factor_inv, sep_sizes):
     width = factor_inv.shape[1]
-    first = EXTRA + B * len(UNITS_FIRST)
-    last = B * len(UNITS_LAST)
+    first = EXTRA + width * len(UNITS_FIRST)
+    last = width * len(UNITS_LAST)
     return pl.pallas_call(
         pack_kernel,
-        out_shape=tuple(pltpu.VMEM((rows, width), jnp.bfloat16) for rows in (first, last, first + last)),
+        out_shape=tuple(jax.ShapeDtypeStruct((rows, B), jnp.bfloat16) for rows in (first, last, first + last)),
         in_specs=[
             pl.BlockSpec(memory_space=pltpu.SMEM),
             pl.BlockSpec(memory_space=pltpu.HBM),
         ],
         out_specs=(pl.BlockSpec(memory_space=pltpu.VMEM),) * 3,
         scratch_shapes=[pltpu.VMEM((width, width), jnp.bfloat16), pltpu.SemaphoreType.DMA((width // B,))],
-        compiler_params=pltpu.CompilerParams(vmem_limit_bytes=57 << 20),
+        compiler_params=pltpu.CompilerParams(vmem_limit_bytes=51 << 20),
         cost_estimate=pl.CostEstimate(flops=4 * width * width, bytes_accessed=3 * width * width, transcendentals=0),
         name="pack",
     )(sep_sizes, factor_inv)
@@ -79,15 +78,16 @@
     i = lax.broadcasted_iota(jnp.int32, (B, B), 0)
     j = lax.broadcasted_iota(jnp.int32, (B, B), 1)
     big = n - 1 - u
-    square = unit[:, big * B:(big + 1) * B].astype(jnp.float32)
+    square = unit[big * B:(big + 1) * B, :].astype(jnp.float32)
     lower = jnp.where(i >= j, square, 0.0).astype(jnp.bfloat16)
-    line = diag[:, u * B:(u + 1) * B].astype(jnp.float32)
+    line = diag[u:u + 1, :].astype(jnp.float32)
     other = jnp.where(i > j, square.T, jnp.where(i == j, line, 0.0)).astype(jnp.bfloat16)
     lo, hi = at
-    if u:
-        g[lo:lo + B, 0:u * B] = unit[:, (big + 1) * B:n * B]
+    for c in range(u):
+        g[lo:lo + B, c * B:(c + 1) * B] = unit[(big + 1 + c) * B:(big + 2 + c) * B, :]
     g[lo:lo + B, u * B:(u + 1) * B] = lower
-    g[hi:hi + B, 0:big * B] = unit[:, 0:big * B]
+    for c in range(big):
+        g[hi:hi + B, c * B:(c + 1) * B] = unit[c * B:(c + 1) * B, :]
     g[hi:hi + B, big * B:(big + 1) * B] = other
 
 
@@ -116,10 +116,11 @@
     for k in range(0, len(panels), 2):
         lo, hi = panels[k], panels[k + 1]
         g[k * B:(k + 1) * B, (lo + 1) * B:(hi + 1) * B] = jnp.zeros((B, (hi - lo) * B), jnp.bfloat16)
-    diag = gathered(part_refs, slice(0, 1))
+    lines = len(units) * n * B
+    diag = gathered(part_refs, slice(lines, lines + EXTRA))
     for u in units:
-        at = EXTRA + B * u
-        place(g, (where[u], where[n - 1 - u]), gathered(part_refs, slice(at, at + B)), u, diag, n)
+        at = u * n * B
+        place(g, (where[u], where[n - 1 - u]), gathered(part_refs, slice(at, at + n * B)), u, diag, n)
     wide = 2 * B
     depths = [(panels[k + 1] + 1) * B for k in range(0, len(panels), 2)]
     for b in range(n // 2):
@@ -172,9 +173,9 @@
         lo, hi = panels[k], panels[k + 1]
         g[k * B:(k + 1) * B, (lo + 1) * B:(hi + 1) * B] = jnp.zeros((B, (hi - lo) * B), jnp.bfloat16)
     for u in UNITS_LAST:
-        at = B * UNITS_LAST.index(u)
-        unit = gathered(last_refs, slice(at, at + B))
-        place(g, (where[u], where[n - 1 - u]), unit, u, first_ref[0:1, :], n)
+        at = n * B * UNITS_LAST.index(u)
+        unit = gathered(last_refs, slice(at, at + n * B))
+        place(g, (where[u], where[n - 1 - u]), unit, u, first_ref[first_ref.shape[0] - EXTRA:, :], n)
     blocks = 4
     wide = n * B // blocks
     cut = [slice(b * wide, (b + 1) * wide) for b in range(blocks)]

time: 68.9 us -> 68.6 us (level)
  no operation moved by 1% of the time
where the time goes in v4:
time: 68.6 us; the launch traced here: 68.3 us
  waiting for transfers between devices  27.5 us (40%)
  starting transfers between devices  22.2 us (32%)
  Pallas kernels  14.2 us (21%)
  local copies, waits for them, and re-layouts  3.66 us (5%)
  between operations  0.8 us (1%)
    ppermute x9, waiting for transfers between devices, moved(): return lax.ppermute(block, ('gx', 'gy', 'gz'), pairs)  27.5 us
    ppermute x9, starting transfers between devices, moved(): return lax.ppermute(block, ('gx', 'gy', 'gz'), pairs)  22.2 us
    pallas_call x3, Pallas kernels, update(): pl.pallas_call(functools.partial(slot_kernel, units, acc is not None, who...  9.65 us
    unnamed x6, local copies, waits for them, and re-layouts  3.66 us
    pallas_call x1, Pallas kernels, last_update(): pl.pallas_call(last_kernel, out_shape=jax.ShapeDtypeStruct((1, width, wid...  2.99 us
    pallas_call x1, Pallas kernels, packed(): pl.pallas_call(pack_kernel, out_shape=tuple((jax.ShapeDtypeStruct((rows,...  1.53 us
  transfers between devices with their start and end apart: 9, of which 2 were waited for; matrix products, arithmetic and copies ran while one was open for 0% of the time, Pallas kernels for 14%

profile of v4, /device:TPU:2, one launch (start us, length us, event | category | flops | bytes accessed | tf_op | source)
XLA Modules:
  0.0 68.3 jit_solution(17745553599763575781)
XLA Ops:
  0.7 1.5 %pack.1 = (bf16[3080,128]{1,0:T(8,128)(2,1)S(1)}, bf16[1024,128]{1,0:T(8,128)(2,1)S(1)}, bf16[4104,128]{1,0:T(8,128)(2,1)S(1)}) custom-call(s32[1,1,1]{2,1,0:T(1,128)S(6)} %copy.4.size_ref, bf16[1,1024,1024]{2,1,0:T(8,128)(2,1)} %f_ref.1), custom_call_target="tpu_custom_call" | custom-call | flops 4194304 | bytes 3145728 | tf_op jit(solution)/shard_map/pack/pallas_call | solution.py:62
  2.2 0.0 copy-start.2
  2.2 0.9 %copy-done.2 = bf16[3080,128]{1,0:T(8,128)(2,1)} copy-done((bf16[3080,128]{1,0:T(8,128)(2,1)}, bf16[3080,128]{1,0:T(8,128)(2,1)S(1)}, u32[]{:S(2)}) %copy-start.2) | copy-done | bytes 788504
  3.1 0.0 collective-permute-start
  3.1 0.7 %collective-permute-start.1 = (bf16[4104,128]{1,0:T(8,128)(2,1)S(1)}, bf16[4104,128]{1,0:T(8,128)(2,1)S(1)}, u32[]{:S(2)}, u32[]{:S(2)}) collective-permute-start(bf16[4104,128]{1,0:T(8,128)(2,1)S(1)} %get-tuple-element.8), channel_id=1, source_target_pairs={{1,17},{2,18},{3,19},{5,21},{6,22},{7,23},{9,25},{10,26},{11,27},{... | collective-permute-start | bytes 3151880 | tf_op jit(solution)/shard_map/ppermute | solution.py:224
  3.8 3.5 %collective-permute-start.2 = (bf16[4104,128]{1,0:T(8,128)(2,1)S(1)}, bf16[4104,128]{1,0:T(8,128)(2,1)S(1)}, u32[]{:S(2)}, u32[]{:S(2)}) collective-permute-start(bf16[4104,128]{1,0:T(8,128)(2,1)S(1)} %get-tuple-element.8), channel_id=1, source_target_pairs={{0,16},{4,20},{8,24},{12,28},{15,31},{16,32},{20,36},{24,40},{28,4... | collective-permute-start | bytes 3151880 | tf_op jit(solution)/shard_map/ppermute | solution.py:224
  7.4 3.2 %collective-permute-start.5 = (bf16[1024,128]{1,0:T(8,128)(2,1)S(1)}, bf16[1024,128]{1,0:T(8,128)(2,1)}, u32[]{:S(2)}, u32[]{:S(2)}) collective-permute-start(bf16[1024,128]{1,0:T(8,128)(2,1)S(1)} %get-tuple-element.10), channel_id=1, source_target_pairs={{4,0},{7,14},{8,1},{11,15},{20,16},{23,30},{24,17},{27,31},{36,32}... | collective-permute-start | bytes 786440 | tf_op jit(solution)/shard_map/ppermute | solution.py:224
  10.5 1.4 %collective-permute-start.7 = (bf16[1024,128]{1,0:T(8,128)(2,1)S(1)}, bf16[1024,128]{1,0:T(8,128)(2,1)}, u32[]{:S(2)}, u32[]{:S(2)}) collective-permute-start(bf16[1024,128]{1,0:T(8,128)(2,1)S(1)} %get-tuple-element.10), channel_id=1, source_target_pairs={{3,15},{12,0},{19,31},{28,16},{35,47},{44,32},{51,63},{60,48},{67,... | collective-permute-start | bytes 786440 | tf_op jit(solution)/shard_map/ppermute | solution.py:224
  11.9 0.0 collective-permute-done.refs_1_
  11.9 10.8 %collective-permute-start.3 = (bf16[3080,128]{1,0:T(8,128)(2,1)}, bf16[3080,128]{1,0:T(8,128)(2,1)S(1)}, u32[]{:S(2)}, u32[]{:S(2)}) collective-permute-start(bf16[3080,128]{1,0:T(8,128)(2,1)} %copy-done.2), channel_id=1, source_target_pairs={{1,2},{2,1},{5,6},{6,5},{9,10},{10,9},{13,14},{14,13},{3,4},{4,3},... | collective-permute-start | bytes 2365448 | tf_op jit(solution)/shard_map/ppermute | solution.py:224
  22.6 0.0 copy-start
  22.7 2.8 %copy-done = bf16[3,1024,1024]{2,1,0:T(8,128)(2,1)S(1)} copy-done((bf16[3,1024,1024]{2,1,0:T(8,128)(2,1)S(1)}, bf16[3,1024,1024]{2,1,0:T(8,128)(2,1)}, u32[]{:S(2)}) %copy-start) | copy-done | bytes 6291480
  25.4 0.0 copy-start.1
  25.4 4.3 %shard_map.37.refs_0_ = f32[1,1024,1024]{2,1,0:T(8,128)S(1)} custom-call(s32[1]{0:T(128)S(6)} %sub.3.which_ref, bf16[3,1024,1024]{2,1,0:T(8,128)(2,1)S(1)} %copy-done, bf16[4104,128]{1,0:T(8,128)(2,1)} %collective-permute-done.refs_1_), custom_call_target="tpu_custom_call" | custom-call | flops 4294967296 | bytes 10485760 | tf_op jit(solution)/shard_map/pallas_call | solution.py:150
  29.7 0.0 collective-permute-done.5
  29.7 0.7 collective-permute-start.4
  30.4 0.0 collective-permute-done.7
  30.4 0.7 collective-permute-start.6
  31.1 0.0 collective-permute-done.1.refs_2_
  31.1 1.3 %collective-permute-start.8 = (bf16[1024,128]{1,0:T(8,128)(2,1)}, bf16[1024,128]{1,0:T(8,128)(2,1)S(1)}, u32[]{:S(2)}, u32[]{:S(2)}) collective-permute-start(bf16[1024,128]{1,0:T(8,128)(2,1)} %collective-permute-done.7), channel_id=1, source_target_pairs={{15,4},{0,11},{31,20},{16,27},{47,36},{32,43},{63,52},{48,59},{79,... | collective-permute-start | bytes 786440 | tf_op jit(solution)/shard_map/ppermute | solution.py:224
  32.4 0.0 collective-permute-done.2.refs_3_
  32.4 0.0 copy-done.1
  32.5 3.0 %shard_map.38.refs_0_ = f32[1,1024,1024]{2,1,0:T(8,128)S(1)} custom-call(s32[1]{0:T(128)} %constant.19.clone.1.which_ref, f32[1,1024,1024]{2,1,0:T(8,128)S(1)} %shard_map.37.refs_0_, bf16[3,1024,1024]{2,1,0:T(8,128)(2,1)S(1)} %copy-done.1, bf16[4104,128]{1,0:T(8,128)(2,1)S(1)} %collective-permute-done.1.refs_2_, ...), custom_call_target="tpu_custom_call" | custom-call | flops 4294967296 | bytes 10485760 | tf_op jit(solution)/shard_map/pallas_call | solution.py:150
  35.4 11.2 %collective-permute-done.3.refs_2_.first_ref = bf16[3080,128]{1,0:T(8,128)(2,1)S(1)} collective-permute-done((bf16[3080,128]{1,0:T(8,128)(2,1)}, bf16[3080,128]{1,0:T(8,128)(2,1)S(1)}, u32[]{:S(2)}, u32[]{:S(2)}) %collective-permute-start.3) | collective-permute-done | bytes 788512 | tf_op jit(solution)/shard_map/ppermute | solution.py:224
  46.6 2.4 %shard_map.39.acc_ref = f32[1,1024,1024]{2,1,0:T(8,128)S(1)} custom-call(s32[1]{0:T(128)} %bitcast.which_ref, f32[1,1024,1024]{2,1,0:T(8,128)S(1)} %shard_map.38.refs_0_, bf16[3,1024,1024]{2,1,0:T(8,128)(2,1)S(1)} %copy-done.1, bf16[3080,128]{1,0:T(8,128)(2,1)S(1)} %collective-permute-done.3.refs_2_.first_ref), custom_call_target="tpu_custom_call" | custom-call | flops 3221225472 | bytes 10485760 | tf_op jit(solution)/shard_map/pallas_call | solution.py:150
  49.0 0.0 collective-permute-done.4.refs_0_.refs_3_.refs_6_.refs_9_
  49.0 0.0 collective-permute-done.6.refs_1_.refs_4_.refs_7_.refs_10_
  49.0 16.3 %collective-permute-done.8.refs_2_.refs_5_.refs_8_.refs_11_ = bf16[1024,128]{1,0:T(8,128)(2,1)S(1)} collective-permute-done((bf16[1024,128]{1,0:T(8,128)(2,1)}, bf16[1024,128]{1,0:T(8,128)(2,1)S(1)}, u32[]{:S(2)}, u32[]{:S(2)}) %collective-permute-start.8) | collective-permute-done | bytes 262176 | tf_op jit(solution)/shard_map/ppermute | solution.py:224
  65.3 3.0 %last.1 = f32[1,1024,1024]{2,1,0:T(8,128)} custom-call(s32[1]{0:T(128)} %bitcast.which_ref, f32[1,1024,1024]{2,1,0:T(8,128)S(1)} %shard_map.39.acc_ref, bf16[3,1024,1024]{2,1,0:T(8,128)(2,1)S(1)} %copy-done.1, bf16[3080,128]{1,0:T(8,128)(2,1)S(1)} %collective-permute-done.3.refs_2_.first_ref, ...), custom_call_target="tpu_custom_call" | custom-call | flops 1073741824 | bytes 10485760 | tf_op jit(solution)/shard_map/last/pallas_call | solution.py:204
Async XLA Ops:
  2.2 0.9 %copy-start.2 = (bf16[3080,128]{1,0:T(8,128)(2,1)}, bf16[3080,128]{1,0:T(8,128)(2,1)S(1)}, u32[]{:S(2)}) copy-start(bf16[3080,128]{1,0:T(8,128)(2,1)S(1)} %get-tuple-element.9) | copy-start | bytes 2365444
  3.1 8.8 %collective-permute-start = (bf16[4104,128]{1,0:T(8,128)(2,1)S(1)}, bf16[4104,128]{1,0:T(8,128)(2,1)}, u32[]{:S(2)}, u32[]{:S(2)}) collective-permute-start(bf16[4104,128]{1,0:T(8,128)(2,1)S(1)} %get-tuple-element.8), channel_id=1, source_target_pairs={{0,1},{1,0},{2,3},{3,2},{4,5},{5,4},{6,7},{7,6},{8,9},{9,8},{10,11... | collective-permute-start | bytes 3151880 | tf_op jit(solution)/shard_map/ppermute | solution.py:224
  3.1 28.1 %collective-permute-start.1 = (bf16[4104,128]{1,0:T(8,128)(2,1)S(1)}, bf16[4104,128]{1,0:T(8,128)(2,1)S(1)}, u32[]{:S(2)}, u32[]{:S(2)}) collective-permute-start(bf16[4104,128]{1,0:T(8,128)(2,1)S(1)} %get-tuple-element.8), channel_id=1, source_target_pairs={{1,17},{2,18},{3,19},{5,21},{6,22},{7,23},{9,25},{10,26},{11,27},{... | collective-permute-start | bytes 3151880 | tf_op jit(solution)/shard_map/ppermute | solution.py:224
  3.8 28.6 %collective-permute-start.2 = (bf16[4104,128]{1,0:T(8,128)(2,1)S(1)}, bf16[4104,128]{1,0:T(8,128)(2,1)S(1)}, u32[]{:S(2)}, u32[]{:S(2)}) collective-permute-start(bf16[4104,128]{1,0:T(8,128)(2,1)S(1)} %get-tuple-element.8), channel_id=1, source_target_pairs={{0,16},{4,20},{8,24},{12,28},{15,31},{16,32},{20,36},{24,40},{28,4... | collective-permute-start | bytes 3151880 | tf_op jit(solution)/shard_map/ppermute | solution.py:224
  7.4 22.4 %collective-permute-start.5 = (bf16[1024,128]{1,0:T(8,128)(2,1)S(1)}, bf16[1024,128]{1,0:T(8,128)(2,1)}, u32[]{:S(2)}, u32[]{:S(2)}) collective-permute-start(bf16[1024,128]{1,0:T(8,128)(2,1)S(1)} %get-tuple-element.10), channel_id=1, source_target_pairs={{4,0},{7,14},{8,1},{11,15},{20,16},{23,30},{24,17},{27,31},{36,32}... | collective-permute-start | bytes 786440 | tf_op jit(solution)/shard_map/ppermute | solution.py:224
  10.5 19.9 %collective-permute-start.7 = (bf16[1024,128]{1,0:T(8,128)(2,1)S(1)}, bf16[1024,128]{1,0:T(8,128)(2,1)}, u32[]{:S(2)}, u32[]{:S(2)}) collective-permute-start(bf16[1024,128]{1,0:T(8,128)(2,1)S(1)} %get-tuple-element.10), channel_id=1, source_target_pairs={{3,15},{12,0},{19,31},{28,16},{35,47},{44,32},{51,63},{60,48},{67,... | collective-permute-start | bytes 786440 | tf_op jit(solution)/shard_map/ppermute | solution.py:224
  11.9 34.7 %collective-permute-start.3 = (bf16[3080,128]{1,0:T(8,128)(2,1)}, bf16[3080,128]{1,0:T(8,128)(2,1)S(1)}, u32[]{:S(2)}, u32[]{:S(2)}) collective-permute-start(bf16[3080,128]{1,0:T(8,128)(2,1)} %copy-done.2), channel_id=1, source_target_pairs={{1,2},{2,1},{5,6},{6,5},{9,10},{10,9},{13,14},{14,13},{3,4},{4,3},... | collective-permute-start | bytes 2365448 | tf_op jit(solution)/shard_map/ppermute | solution.py:224
  22.6 2.8 %copy-start = (bf16[3,1024,1024]{2,1,0:T(8,128)(2,1)S(1)}, bf16[3,1024,1024]{2,1,0:T(8,128)(2,1)}, u32[]{:S(2)}) copy-start(bf16[3,1024,1024]{2,1,0:T(8,128)(2,1)} %c_ref.1) | copy-start | bytes 18874372
  25.4 7.0 %copy-start.1 = (bf16[3,1024,1024]{2,1,0:T(8,128)(2,1)S(1)}, bf16[3,1024,1024]{2,1,0:T(8,128)(2,1)}, u32[]{:S(2)}) copy-start(bf16[3,1024,1024]{2,1,0:T(8,128)(2,1)} %c_ref.1) | copy-start | bytes 18874372
  29.7 19.3 %collective-permute-start.4 = (bf16[1024,128]{1,0:T(8,128)(2,1)S(1)}, bf16[1024,128]{1,0:T(8,128)(2,1)S(1)}, u32[]{:S(2)}, u32[]{:S(2)}) collective-permute-start(bf16[1024,128]{1,0:T(8,128)(2,1)S(1)} %get-tuple-element.10), channel_id=1, source_target_pairs={{1,2},{2,1},{5,6},{6,5},{9,10},{10,9},{13,14},{14,13},{17,18},{18,... | collective-permute-start | bytes 786440 | tf_op jit(solution)/shard_map/ppermute | solution.py:224
  30.4 18.6 %collective-permute-start.6 = (bf16[1024,128]{1,0:T(8,128)(2,1)}, bf16[1024,128]{1,0:T(8,128)(2,1)S(1)}, u32[]{:S(2)}, u32[]{:S(2)}) collective-permute-start(bf16[1024,128]{1,0:T(8,128)(2,1)} %collective-permute-done.5), channel_id=1, source_target_pairs={{0,3},{14,8},{1,7},{15,12},{16,19},{30,24},{17,23},{31,28},{32,35}... | collective-permute-start | bytes 786440 | tf_op jit(solution)/shard_map/ppermute | solution.py:224
  31.1 34.2 %collective-permute-start.8 = (bf16[1024,128]{1,0:T(8,128)(2,1)}, bf16[1024,128]{1,0:T(8,128)(2,1)S(1)}, u32[]{:S(2)}, u32[]{:S(2)}) collective-permute-start(bf16[1024,128]{1,0:T(8,128)(2,1)} %collective-permute-done.7), channel_id=1, source_target_pairs={{15,4},{0,11},{31,20},{16,27},{47,36},{32,43},{63,52},{48,59},{79,... | collective-permute-start | bytes 786440 | tf_op jit(solution)/shard_map/ppermute | solution.py:224
